TPU v7x, 1024 devices: a whole 4x8x16 slice. The times are simulated.
1024 devices in a mesh: panel: 8 (over y), tile: 32 (over z, core), lev: 4 (over x).
Axes of the slice: x: 4, y: 8, z: 16, core: 2. Of those that a mesh axis runs over, the one named last changes fastest.
Arguments:
- adjoint_new: float32 [5, 32, 524288], P(None, 'lev', ('panel', 'tile')), may hold values from -6 to 6
- weights: float32 [4, 524288], P(None, ('panel', 'tile', 'lev')), may hold values from 0.05 to 0.5
- departure: int32 [4, 524288], P(None, ('panel', 'tile')), may hold values from 0 to 2047
- send_point: int32 [4, 32768], P(None, ('panel', 'tile')), may hold values from 0 to 8191, as said below
- block_count: int32 [4, 256], P(None, ('panel', 'tile')), may hold values from 0 to 128, as said below
- rotation: int32 [2, 256], P(None, ('panel', 'tile')), may hold values from 0 to 3
Outputs:
- adjoint_old: float32 [5, 32, 524288], P(None, 'lev', ('panel', 'tile'))
Inputs may be any that keep to these rules, and one draw needn't show every extreme that they name: `send_point`: within one tile the 512 entries are distinct stencil point numbers k * 2048 + c of that tile's own cells. `block_count`: zero for block 0 on the first tile and for block 1 on the last tile of each sector; every block position reaches 128 on some tile in every draw.
All inputs are finite; a program needn't handle non-finite values.
Results may differ from a plain program's by a relative error of at most 0.00002.
Values sent between devices are 32-bit elements; how exact they have to be, the bound alone decides.
A program may use at most 32 MiB of HBM per device.

v0:
```python
import jax
import jax.numpy as jnp
from jax import lax
from jax.sharding import PartitionSpec as P


def laid_out(parts, dim):
    lengths = list(parts.shape[1:])
    lengths[dim] *= parts.shape[0]
    return jnp.moveaxis(parts, 0, dim).reshape(lengths)


def from_everyone(array, axis):
    devices = lax.axis_size(axis)
    return lax.all_to_all(
        jnp.broadcast_to(array[None], (devices, *array.shape)), axis, 0, 0, tiled=True
    )


def collect(array, axis, dim):
    return laid_out(from_everyone(array, axis), dim)


def shifted(block, axis, distance):
    devices = range(lax.axis_size(axis))
    route = [(i - distance, i) for i in devices if i - distance in devices]
    return lax.ppermute(block, axis, route)


def shifted_2(value, axis, steps):
    count = lax.axis_size(axis)
    pairs = [(source, (source + steps) % count) for source in range(count)]
    return lax.ppermute(value, axis, pairs)


def quarter_turn(turn_code):
    cosine = (turn_code == 0).astype(jnp.float32) - (turn_code == 2).astype(jnp.float32)
    sine_term = (turn_code == 1).astype(jnp.float32) - (turn_code == 3).astype(jnp.float32)
    return (cosine, sine_term)


def body(adjoint_new, weights, departure, send_point, block_count, rotation):
    fields, levels, cell_count = adjoint_new.shape
    blocks, slot_count = send_point.shape
    stencil = departure.shape[0]
    row_count = fields * levels
    points = stencil * cell_count
    weight_full = collect(weights, "lev", 1)
    weighted = (adjoint_new[:, :, None, :] * weight_full[None, None, :, :]).reshape(
        row_count, points
    )
    chosen = send_point.reshape(-1)
    live_mask = lax.broadcasted_iota(jnp.int32, (blocks, slot_count), 1) < block_count
    picked = weighted[:, chosen].reshape(fields, levels, blocks, slot_count) * live_mask.astype(
        jnp.float32
    )
    cosine, sine_term = quarter_turn(rotation)
    zonal_part = picked[0, :, 2:, :]
    merid_part = picked[1, :, 2:, :]
    turned_zonal = cosine * zonal_part + sine_term * merid_part
    turned_merid = cosine * merid_part - sine_term * zonal_part
    wind_rows = jnp.stack(
        [
            jnp.concatenate([picked[0, :, :2, :], turned_zonal], axis=1),
            jnp.concatenate([picked[1, :, :2, :], turned_merid], axis=1),
        ]
    )
    outgoing = jnp.concatenate([wind_rows, picked[2:]], axis=0).reshape(
        row_count, blocks, slot_count
    )
    targets = departure.reshape(-1)[chosen].reshape(blocks, slot_count)
    dropped = jnp.where(live_mask, send_point, points).reshape(-1)
    keep_local = jnp.ones((points,), jnp.float32).at[dropped].set(0.0, mode="drop")
    result = (
        jnp.zeros((row_count, cell_count), jnp.float32)
        .at[:, departure.reshape(-1)]
        .add(weighted * keep_local)
    )
    from_before = shifted((outgoing[:, 1], targets[1]), "tile", 1)
    from_beyond = shifted((outgoing[:, 0], targets[0]), "tile", -1)
    seam_before = shifted_2((outgoing[:, 3], targets[3]), "panel", 1)
    seam_beyond = shifted_2((outgoing[:, 2], targets[2]), "panel", -1)
    received = (from_before, from_beyond, seam_before, seam_beyond)
    arrived = jnp.concatenate([member[0] for member in received], axis=1)
    arrived_ids = jnp.concatenate([member[1] for member in received])
    result = result.at[:, arrived_ids].add(arrived)
    return result.reshape(fields, levels, cell_count)


def solution(mesh):
    return jax.shard_map(
        body,
        mesh=mesh,
        in_specs=(
            P(None, "lev", ("panel", "tile")),
            P(None, ("panel", "tile", "lev")),
            P(None, ("panel", "tile")),
            P(None, ("panel", "tile")),
            P(None, ("panel", "tile")),
            P(None, ("panel", "tile")),
        ),
        out_specs=P(None, "lev", ("panel", "tile")),
        check_vma=False,
    )
```

profile of v0, /device:TPU:1, one launch (start us, length us, event | category | flops | bytes accessed | tf_op | source)
XLA Modules:
  0.0 109.1 jit_solution(6483425726398444044)
XLA Ops:
  0.0 1.4 %broadcast_in_dim.12 = f32[4,4,512]{2,1,0:T(4,128)} broadcast(f32[4,512]{1,0:T(4,128)} %param.7), dimensions={1,2} | broadcast | bytes 40960 | tf_op jit(solution)/shard_map/broadcast_in_dim | solution.py:16
  1.4 4.8 %all-to-all-start = ((f32[4,4,512]{2,1,0:T(4,128)}), f32[4,4,512]{2,1,0:T(4,128)S(1)}, u32[]{:S(2)}, u32[]{:S(2)}) async-start(f32[4,4,512]{2,1,0:T(4,128)} %broadcast_in_dim.12), calls=%async_computation | async-start | bytes 65536 | tf_op jit(solution)/shard_map/all_to_all | solution.py:15
  6.2 0.7 compare_select_fusion.2
  6.9 0.8 copy.35
  7.7 3.1 %gather_fusion = s32[512]{0:T(512)S(1)} fusion(s32[8192]{0:T(1024)S(1)} %bitcast.68, s32[1024]{0:T(1024)S(1)} %pad_clamp_fusion), kind=kCustom, calls=%fused_computation | custom fusion | bytes 6144 | tf_op jit(solution)/shard_map/gather | solution.py:71
  10.8 3.2 %collective-permute-start.2 = (s32[128]{0:T(128)S(1)}, s32[128]{0:T(128)S(1)}, u32[]{:S(2)}, u32[]{:S(2)}) collective-permute-start(s32[128]{0:T(128)S(1)} %get-tuple-element.16), channel_id=1, source_target_pairs={{0,128},{128,256},{256,384},{384,512},{512,640},{640,768},{768,896... | collective-permute-start | bytes 1544 | tf_op jit(solution)/shard_map/ppermute | solution.py:33
  14.1 3.8 %collective-permute-start.3 = (s32[128]{0:T(128)S(1)}, s32[128]{0:T(128)S(1)}, u32[]{:S(2)}, u32[]{:S(2)}) collective-permute-start(s32[128]{0:T(128)S(1)} %get-tuple-element.18), channel_id=1, source_target_pairs={{0,896},{128,0},{256,128},{384,256},{512,384},{640,512},{768,640},... | collective-permute-start | bytes 1544 | tf_op jit(solution)/shard_map/ppermute | solution.py:33
  17.9 5.1 %collective-permute-start = (s32[128]{0:T(128)S(1)}, s32[128]{0:T(128)S(1)}, u32[]{:S(2)}, u32[]{:S(2)}) collective-permute-start(s32[128]{0:T(128)S(1)} %get-tuple-element.15), channel_id=1, source_target_pairs={{0,4},{4,8},{8,12},{12,16},{16,20},{20,24},{24,28},{28,32},{32,36}... | collective-permute-start | bytes 1544 | tf_op jit(solution)/shard_map/ppermute | solution.py:27
  23.0 10.7 %collective-permute-start.1 = (s32[128]{0:T(128)S(1)}, s32[128]{0:T(128)S(1)}, u32[]{:S(2)}, u32[]{:S(2)}) collective-permute-start(s32[128]{0:T(128)S(1)} %get-tuple-element.17), channel_id=1, source_target_pairs={{4,0},{8,4},{12,8},{16,12},{20,16},{24,20},{28,24},{32,28},{36,32}... | collective-permute-start | bytes 1544 | tf_op jit(solution)/shard_map/ppermute | solution.py:27
  33.8 0.3 broadcast_bitcast_fusion
  34.3 0.7 copy.33
  35.1 2.5 %scatter_custom_fusion = f32[8192]{0:T(1024)S(1)} fusion(s32[512]{0:T(512)S(1)} %bitcast.84, f32[512]{0:T(512)S(1)} %broadcast.91, f32[]{:T(128)} %constant.11.clone.1), kind=kCustom, calls=%fused_computation.22 | custom fusion | bytes 32772 | tf_op jit(solution)/shard_map/scatter | solution.py:73
  37.6 1.3 %multiply_bitcast_fusion = (f32[8192,40]{0,1:T(8,128)S(1)}, f32[40,8192]{1,0:T(8,128)}) fusion(f32[8192]{0:T(1024)S(1)} %scatter_custom_fusion, f32[40,8192]{1,0:T(8,128)S(1)} %bitcast.69, f32[8192]{0:T(1024)S(1)} %bitcast.71), kind=kLoop, calls=%fused_computation.5 | loop fusion | flops 655360 | bytes 3997696 | tf_op jit(solution)/shard_map/mul | solution.py:77
  38.9 3.6 %copy.27 = f32[40,8192]{0,1:T(8,128)} copy(f32[40,8192]{1,0:T(8,128)} %get-tuple-element.6) | data formatting | bytes 2621440 | tf_op jit(solution)/shard_map/mul | solution.py:49
  42.6 3.2 %gather_fusion.1 = f32[512,40]{1,0:T(8,128)S(1)} fusion(f32[40,8192]{0,1:T(8,128)} %copy.27, s32[1024]{0:T(1024)S(1)} %pad_clamp_fusion), kind=kCustom, calls=%fused_computation.1 | custom fusion | bytes 165888 | tf_op jit(solution)/shard_map/gather | solution.py:54
  46.0 1.9 %collective-permute-start.4 = (f32[40,128]{1,0:T(8,128)S(1)}, f32[40,128]{1,0:T(8,128)S(1)}, u32[]{:S(2)}, u32[]{:S(2)}) collective-permute-start(f32[40,128]{1,0:T(8,128)S(1)} %get-tuple-element.9), channel_id=1, source_target_pairs={{0,4},{4,8},{8,12},{12,16},{16,20},{20,24},{24,28},{28,32},{32,36}... | collective-permute-start | bytes 61448 | tf_op jit(solution)/shard_map/ppermute | solution.py:27
  48.0 2.4 %collective-permute-start.5 = (f32[40,128]{1,0:T(8,128)S(1)}, f32[40,128]{1,0:T(8,128)S(1)}, u32[]{:S(2)}, u32[]{:S(2)}) collective-permute-start(f32[40,128]{1,0:T(8,128)S(1)} %get-tuple-element.12), channel_id=1, source_target_pairs={{4,0},{8,4},{12,8},{16,12},{20,16},{24,20},{28,24},{32,28},{36,32}... | collective-permute-start | bytes 61448 | tf_op jit(solution)/shard_map/ppermute | solution.py:27
  50.4 1.9 %collective-permute-start.6 = (f32[40,128]{1,0:T(8,128)S(1)}, f32[40,128]{1,0:T(8,128)S(1)}, u32[]{:S(2)}, u32[]{:S(2)}) collective-permute-start(f32[40,128]{1,0:T(8,128)S(1)} %get-tuple-element.11), channel_id=1, source_target_pairs={{0,128},{128,256},{256,384},{384,512},{512,640},{640,768},{768,896... | collective-permute-start | bytes 61448 | tf_op jit(solution)/shard_map/ppermute | solution.py:33
  52.3 4.6 %collective-permute-start.7 = (f32[40,128]{1,0:T(8,128)S(1)}, f32[40,128]{1,0:T(8,128)S(1)}, u32[]{:S(2)}, u32[]{:S(2)}) collective-permute-start(f32[40,128]{1,0:T(8,128)S(1)} %get-tuple-element.10), channel_id=1, source_target_pairs={{0,896},{128,0},{256,128},{384,256},{512,384},{640,512},{768,640},... | collective-permute-start | bytes 61448 | tf_op jit(solution)/shard_map/ppermute | solution.py:33
  56.9 2.7 %copy.26 = f32[8192,40]{1,0:T(8,128)} copy(f32[8192,40]{0,1:T(8,128)S(1)} %get-tuple-element.5) | data formatting | bytes 2621440 | tf_op jit(solution)/shard_map/mul | solution.py:77
  59.6 44.6 %scatter_custom_fusion.1 = f32[40,2048]{0,1:T(8,128)S(1)} fusion(s32[8192]{0:T(1024)S(1)} %bitcast.77, f32[8192,40]{1,0:T(8,128)} %copy.26, f32[]{:T(128)} %constant.8.clone.1), kind=kCustom, calls=%fused_computation.8 | custom fusion | flops 327680 | bytes 328192 | tf_op jit(solution)/shard_map/scatter-add | solution.py:77
  104.2 0.1 copy.30
  104.4 3.7 %scatter_fusion = f32[40,2048]{0,1:T(8,128)S(1)} fusion(f32[40,2048]{0,1:T(8,128)S(1)} %scatter_custom_fusion.1, s32[512]{0:T(512)S(1)} %bitcast.78, f32[512,40]{1,0:T(8,128)S(1)} %copy.30), kind=kCustom, calls=%fused_computation.4 | custom fusion | flops 20480 | bytes 247808 | tf_op jit(solution)/shard_map/scatter-add | solution.py:86
  108.1 1.0 copy.31
  (40 shorter events, 0.6 us)
Async XLA Ops:
  0.0 33.8 %copy-start = (f32[5,8,2048]{2,1,0:T(8,128)S(1)}, f32[5,8,2048]{2,1,0:T(8,128)}, u32[]{:S(2)}) copy-start(f32[5,8,2048]{2,1,0:T(8,128)} %param.6) | copy-start | bytes 983044
  0.0 33.7 %copy-start.2 = (s32[4,128]{1,0:T(4,128)S(1)}, s32[4,128]{1,0:T(4,128)}, u32[]{:S(2)}) copy-start(s32[4,128]{1,0:T(4,128)} %param.9) | copy-start | bytes 6148
  0.0 33.7 %copy-start.3 = (s32[4,1]{0,1:T(1,128)S(1)}, s32[4,1]{0,1:T(1,128)}, u32[]{:S(2)}) copy-start(s32[4,1]{0,1:T(1,128)} %param.10) | copy-start | bytes 52
  1.4 36.2 %all-to-all-start = ((f32[4,4,512]{2,1,0:T(4,128)}), f32[4,4,512]{2,1,0:T(4,128)S(1)}, u32[]{:S(2)}, u32[]{:S(2)}) async-start(f32[4,4,512]{2,1,0:T(4,128)} %broadcast_in_dim.12), calls=%async_computation | async-start | bytes 65536 | tf_op jit(solution)/shard_map/all_to_all | solution.py:15
  10.8 23.4 %copy-start.1 = (s32[4,2048]{1,0:T(4,128)S(1)}, s32[4,2048]{1,0:T(4,128)}, u32[]{:S(2)}) copy-start(s32[4,2048]{1,0:T(4,128)} %param.8) | copy-start | bytes 98308
  10.8 23.5 %copy-start.4 = (s32[2,1]{0,1:T(1,128)S(1)}, s32[2,1]{0,1:T(1,128)}, u32[]{:S(2)}) copy-start(s32[2,1]{0,1:T(1,128)} %param.11) | copy-start | bytes 28
  10.8 37.1 %collective-permute-start.2 = (s32[128]{0:T(128)S(1)}, s32[128]{0:T(128)S(1)}, u32[]{:S(2)}, u32[]{:S(2)}) collective-permute-start(s32[128]{0:T(128)S(1)} %get-tuple-element.16), channel_id=1, source_target_pairs={{0,128},{128,256},{256,384},{384,512},{512,640},{640,768},{768,896... | collective-permute-start | bytes 1544 | tf_op jit(solution)/shard_map/ppermute | solution.py:33
  14.1 36.3 %collective-permute-start.3 = (s32[128]{0:T(128)S(1)}, s32[128]{0:T(128)S(1)}, u32[]{:S(2)}, u32[]{:S(2)}) collective-permute-start(s32[128]{0:T(128)S(1)} %get-tuple-element.18), channel_id=1, source_target_pairs={{0,896},{128,0},{256,128},{384,256},{512,384},{640,512},{768,640},... | collective-permute-start | bytes 1544 | tf_op jit(solution)/shard_map/ppermute | solution.py:33
  17.9 34.5 %collective-permute-start = (s32[128]{0:T(128)S(1)}, s32[128]{0:T(128)S(1)}, u32[]{:S(2)}, u32[]{:S(2)}) collective-permute-start(s32[128]{0:T(128)S(1)} %get-tuple-element.15), channel_id=1, source_target_pairs={{0,4},{4,8},{8,12},{12,16},{16,20},{20,24},{24,28},{28,32},{32,36}... | collective-permute-start | bytes 1544 | tf_op jit(solution)/shard_map/ppermute | solution.py:27
  23.0 33.9 %collective-permute-start.1 = (s32[128]{0:T(128)S(1)}, s32[128]{0:T(128)S(1)}, u32[]{:S(2)}, u32[]{:S(2)}) collective-permute-start(s32[128]{0:T(128)S(1)} %get-tuple-element.17), channel_id=1, source_target_pairs={{4,0},{8,4},{12,8},{16,12},{20,16},{24,20},{28,24},{32,28},{36,32}... | collective-permute-start | bytes 1544 | tf_op jit(solution)/shard_map/ppermute | solution.py:27
  46.0 58.1 %collective-permute-start.4 = (f32[40,128]{1,0:T(8,128)S(1)}, f32[40,128]{1,0:T(8,128)S(1)}, u32[]{:S(2)}, u32[]{:S(2)}) collective-permute-start(f32[40,128]{1,0:T(8,128)S(1)} %get-tuple-element.9), channel_id=1, source_target_pairs={{0,4},{4,8},{8,12},{12,16},{16,20},{20,24},{24,28},{28,32},{32,36}... | collective-permute-start | bytes 61448 | tf_op jit(solution)/shard_map/ppermute | solution.py:27
  48.0 56.2 %collective-permute-start.5 = (f32[40,128]{1,0:T(8,128)S(1)}, f32[40,128]{1,0:T(8,128)S(1)}, u32[]{:S(2)}, u32[]{:S(2)}) collective-permute-start(f32[40,128]{1,0:T(8,128)S(1)} %get-tuple-element.12), channel_id=1, source_target_pairs={{4,0},{8,4},{12,8},{16,12},{20,16},{24,20},{28,24},{32,28},{36,32}... | collective-permute-start | bytes 61448 | tf_op jit(solution)/shard_map/ppermute | solution.py:27
  50.4 53.8 %collective-permute-start.6 = (f32[40,128]{1,0:T(8,128)S(1)}, f32[40,128]{1,0:T(8,128)S(1)}, u32[]{:S(2)}, u32[]{:S(2)}) collective-permute-start(f32[40,128]{1,0:T(8,128)S(1)} %get-tuple-element.11), channel_id=1, source_target_pairs={{0,128},{128,256},{256,384},{384,512},{512,640},{640,768},{768,896... | collective-permute-start | bytes 61448 | tf_op jit(solution)/shard_map/ppermute | solution.py:33
  52.3 51.9 %collective-permute-start.7 = (f32[40,128]{1,0:T(8,128)S(1)}, f32[40,128]{1,0:T(8,128)S(1)}, u32[]{:S(2)}, u32[]{:S(2)}) collective-permute-start(f32[40,128]{1,0:T(8,128)S(1)} %get-tuple-element.10), channel_id=1, source_target_pairs={{0,896},{128,0},{256,128},{384,256},{512,384},{640,512},{768,640},... | collective-permute-start | bytes 61448 | tf_op jit(solution)/shard_map/ppermute | solution.py:33
where the time goes:
time: 110 us; the launch traced here: 109 us
  other arithmetic  50.5 us (46%)
  starting transfers between devices  38.5 us (35%)
  local copies, waits for them, and re-layouts  19.7 us (18%)
    scatter-add x1, other arithmetic, body(): result = jnp.zeros((row_count, cell_count), jnp.float32).at[:, departure....  44.6 us
    ppermute x4, starting transfers between devices, shifted(): return lax.ppermute(block, axis, route)  20.1 us
    ppermute x4, starting transfers between devices, shifted_2(): return lax.ppermute(value, axis, pairs)  13.5 us
    all_to_all x1, starting transfers between devices, from_everyone(): lax.all_to_all(jnp.broadcast_to(array[None], (devices, *array.shape)), ax...  4.83 us
    scatter-add x1, other arithmetic, body(): result = result.at[:, arrived_ids].add(arrived)  3.69 us
    mul x1, local copies, waits for them, and re-layouts, body(): adjoint_new[:, :, None, :] * weight_full[None, None, :, :]  3.65 us
    gather x2, local copies, waits for them, and re-layouts, body(): weighted[:, chosen].reshape(fields, levels, blocks, slot_count)  3.32 us
    gather x1, local copies, waits for them, and re-layouts, body(): targets = departure.reshape(-1)[chosen].reshape(blocks, slot_count)  3.13 us
  transfers between devices with their start and end apart: 9, of which 0 were waited for; matrix products, arithmetic and copies ran while one was open for 59% of the time, Pallas kernels for 0%

commit v1 on v0

v1 whole, which is shorter than its diff:
```python
import functools

import jax
import jax.numpy as jnp
from jax import lax
from jax.experimental import pallas as pl
from jax.experimental.pallas import tpu as pltpu
from jax.sharding import PartitionSpec as P

MESH = pl.DeviceIdType.MESH
LOW = 256
F32, BF16, I32 = jnp.float32, jnp.bfloat16, jnp.int32


def split_rows(value):
    high = value.astype(BF16).astype(F32)
    return jnp.concatenate([high, value - high], axis=0).astype(BF16)


def one_hot(low, columns):
    rows = lax.broadcasted_iota(I32, (LOW, columns), 0)
    return jnp.where(rows == low, 1.0, 0.0).astype(BF16)


def times_transposed(lhs, rhs):
    return lax.dot_general(lhs, rhs, (((1,), (1,)), ((), ())), preferred_element_type=F32)


def spread(value, target_high, target_low, groups):
    parts = split_rows(value)
    copies = parts.shape[0] // 16
    high = jnp.broadcast_to(target_high, (16, LOW))
    lhs = []
    for g in range(groups):
        mask = jnp.where(high == g, 1.0, 0.0).astype(BF16)
        lhs.append(parts * jnp.concatenate([mask] * copies, axis=0))
    return times_transposed(jnp.concatenate(lhs, axis=0), one_hot(target_low, LOW))


def kernel(
    sizes,
    x_hbm,
    w_hbm,
    dep_hbm,
    sp_hbm,
    count_ref,
    turn_ref,
    out_ref,
    x,
    w,
    dep,
    sp,
    hot,
    glhs,
    sent,
    picked,
    acc,
    pay,
    recv,
    in_sem,
    w_send,
    w_recv,
    p_send,
    p_recv,
):
    n_panel, n_tile, n_lev = sizes
    fields, levels, cells = x.shape
    stencil = dep.shape[0]
    blocks, slots = sp.shape
    rows = fields * levels
    groups = cells // LOW
    share = cells // n_lev
    per_lev = share // LOW
    panel, tile, lev = (lax.axis_index(a) for a in ("panel", "tile", "lev"))
    shift_cell = cells.bit_length() - 1
    shift_low = LOW.bit_length() - 1

    loads = [
        pltpu.make_async_copy(src, dst, in_sem.at[i])
        for i, (src, dst) in enumerate(((w_hbm, w.at[0]), (sp_hbm, sp), (dep_hbm, dep), (x_hbm, x)))
    ]
    for load in loads:
        load.start()

    barrier = pltpu.get_barrier_semaphore()

    def greet(device):
        pl.semaphore_signal(barrier, inc=1, device_id=device, device_id_type=MESH)

    has_prev, has_next = tile > 0, tile < n_tile - 1
    next_panel, prev_panel = lax.rem(panel + 1, n_panel), lax.rem(panel + n_panel - 1, n_panel)
    for d in range(1, n_lev):
        greet({"lev": lax.rem(lev + d, n_lev)})
    greet({"panel": prev_panel})
    greet({"panel": next_panel})

    @pl.when(has_prev)
    def _():
        greet({"tile": tile - 1})

    @pl.when(has_next)
    def _():
        greet({"tile": tile + 1})

    loads[0].wait()
    pl.semaphore_wait(barrier, n_lev + 1 + has_prev.astype(I32) + has_next.astype(I32))

    w_copies = [
        pltpu.make_async_remote_copy(
            src_ref=w.at[0],
            dst_ref=w.at[n_lev - d],
            send_sem=w_send.at[d - 1],
            recv_sem=w_recv.at[n_lev - d - 1],
            device_id={"lev": lax.rem(lev + d, n_lev)},
            device_id_type=MESH,
        )
        for d in range(1, n_lev)
    ]
    for copy in w_copies:
        copy.start()

    loads[1].wait()
    loads[2].wait()
    loads[3].wait()

    point = [sp[j : j + 1, :] for j in range(blocks)]
    cell_high = [(p & (cells - 1)) >> shift_low for p in point]
    stencil_of = [p >> shift_cell for p in point]
    lane = lax.broadcasted_iota(I32, (1, slots), 1)
    live = [lane < count_ref[j] for j in range(blocks)]
    for j in range(blocks):
        hot[:, j * slots : (j + 1) * slots] = one_hot(point[j] & (LOW - 1), slots)

    number = lax.broadcasted_iota(I32, (stencil * groups, slots), 0)
    marks = [
        jnp.where((number == (point[j] >> shift_low)) & live[j], 1.0, 0.0).astype(BF16)
        for j in range(blocks)
    ]
    sent[...] = times_transposed(jnp.concatenate(marks, axis=1), hot[...])

    height = 2 * rows + 16
    for g in range(groups):
        part = x[:, :, g * LOW : (g + 1) * LOW].reshape(rows, LOW)
        d4 = dep[:, g * LOW : (g + 1) * LOW]
        d8 = jnp.concatenate([d4 >> shift_low, d4 & (LOW - 1)], axis=0).astype(F32)
        d16 = jnp.concatenate([d8, jnp.zeros((8, LOW), F32)], axis=0).astype(BF16)
        glhs[g * height : g * height + 2 * rows, :] = split_rows(part)
        glhs[g * height + 2 * rows : (g + 1) * height, :] = d16
    row8 = lax.broadcasted_iota(I32, (8, slots), 0)
    for n in range(blocks * slots // LOW):
        found = jnp.dot(glhs[...], hot[:, n * LOW : (n + 1) * LOW], preferred_element_type=F32)
        for i in range(LOW // slots):
            j = n * (LOW // slots) + i
            total = jnp.zeros((height, slots), F32)
            for g in range(groups):
                piece = found[g * height : (g + 1) * height, i * slots : (i + 1) * slots]
                total = total + jnp.where(cell_high[j] == g, piece, 0.0)
            picked[j] = total[:rows] + total[rows : 2 * rows]
            scale = jnp.where(row8 < stencil, float(LOW), 1.0)
            own = (row8 & (stencil - 1)) == stencil_of[j]
            target = jnp.sum(
                jnp.where(own, total[2 * rows : 2 * rows + 8] * scale, 0.0), axis=0, keepdims=True
            )
            pay[j, rows : rows + 8, :] = jnp.broadcast_to(target, (8, slots))

    def segment(d):
        first = lax.rem(lev + d, n_lev)
        result = None
        for i in range(per_lev):
            at = pl.ds(pl.multiple_of(first * share + i * LOW, LOW), LOW)
            part = x[:, :, at].reshape(rows, LOW)
            for k in range(stencil):
                weight = w[d, k : k + 1, i * LOW : (i + 1) * LOW]
                landing = dep[k : k + 1, at]
                gone = sent[pl.ds(k * groups + first * per_lev + i, 1), :]
                high = jnp.where(gone > 0.5, groups, landing >> shift_low)
                term = spread(part * weight, high, landing & (LOW - 1), groups)
                result = term if result is None else result + term
        return result

    acc[...] = segment(0)

    for copy in w_copies:
        copy.wait_recv()

    wlhs = []
    for d in range(n_lev):
        for i in range(per_lev):
            w4 = w[d, :, i * LOW : (i + 1) * LOW]
            b1 = w4.astype(BF16).astype(F32)
            b2 = (w4 - b1).astype(BF16).astype(F32)
            wlhs.append(
                jnp.concatenate([b1, b2, w4 - b1 - b2, jnp.zeros_like(w4)], axis=0).astype(BF16)
            )
    found = jnp.dot(jnp.concatenate(wlhs, axis=0), hot[...], preferred_element_type=F32)
    row16 = lax.broadcasted_iota(I32, (16, slots), 0)
    for j in range(blocks):
        total = jnp.zeros((16, slots), F32)
        for d in range(n_lev):
            for i in range(per_lev):
                r = d * per_lev + i
                g = lax.rem(lev + d, n_lev) * per_lev + i
                piece = found[r * 16 : (r + 1) * 16, j * slots : (j + 1) * slots]
                total = total + jnp.where(cell_high[j] == g, piece, 0.0)
        own = (row16 & (stencil - 1)) == stencil_of[j]
        weight = jnp.sum(jnp.where(own, total, 0.0), axis=0, keepdims=True)
        weight = jnp.where(live[j], weight, 0.0)
        value = picked[j] * weight
        if j >= 2:
            code = turn_ref[j - 2]
            cosine = jnp.where(code == 0, 1.0, 0.0) - jnp.where(code == 2, 1.0, 0.0)
            sine = jnp.where(code == 1, 1.0, 0.0) - jnp.where(code == 3, 1.0, 0.0)
            zonal, merid = value[:levels], value[levels : 2 * levels]
            value = jnp.concatenate(
                [cosine * zonal + sine * merid, cosine * merid - sine * zonal, value[2 * levels :]],
                axis=0,
            )
        pay[j, 0:rows, :] = value

    def block_copy(j, device):
        return pltpu.make_async_remote_copy(
            src_ref=pay.at[j],
            dst_ref=recv.at[j],
            send_sem=p_send.at[j],
            recv_sem=p_recv.at[j],
            device_id=device,
            device_id_type=MESH,
        )

    copies = [
        block_copy(0, {"tile": jnp.maximum(tile - 1, 0)}),
        block_copy(1, {"tile": jnp.minimum(tile + 1, n_tile - 1)}),
        block_copy(2, {"panel": prev_panel}),
        block_copy(3, {"panel": next_panel}),
    ]

    @pl.when(has_prev)
    def _():
        copies[0].start()

    @pl.when(has_next)
    def _():
        copies[1].start()

    copies[2].start()
    copies[3].start()

    for d in (1, 3, 2):
        acc[...] += segment(d)

    for j, (there, here) in enumerate(((has_prev, has_next), (has_next, has_prev))):

        @pl.when(here)
        def _():
            copies[j].wait_recv()

        @pl.when(jnp.logical_not(here))
        def _():
            recv[j] = jnp.zeros_like(recv[j])

    copies[2].wait_recv()
    copies[3].wait_recv()

    result = acc[...]
    for n in range(blocks * slots // LOW):
        pair = [recv[n * (LOW // slots) + i] for i in range(LOW // slots)]
        value = jnp.concatenate([p[:rows] for p in pair], axis=1)
        landing = jnp.concatenate([p[rows : rows + 1] for p in pair], axis=1).astype(I32)
        result = result + spread(value, landing >> shift_low, landing & (LOW - 1), groups)
    for g in range(groups):
        top = g * 2 * rows
        out_ref[:, :, g * LOW : (g + 1) * LOW] = (
            result[top : top + rows] + result[top + rows : top + 2 * rows]
        ).reshape(fields, levels, LOW)

    for copy in w_copies:
        copy.wait_send()
    for j, there in enumerate((has_prev, has_next)):

        @pl.when(there)
        def _():
            copies[j].wait_send()

    copies[2].wait_send()
    copies[3].wait_send()


def body(sizes, adjoint_new, weights, departure, send_point, block_count, rotation):
    fields, levels, cells = adjoint_new.shape
    stencil = departure.shape[0]
    blocks, slots = send_point.shape
    rows = fields * levels
    groups = cells // LOW
    n_lev = sizes[2]
    hbm = pl.BlockSpec(memory_space=pl.ANY)
    smem = pl.BlockSpec(memory_space=pltpu.SMEM)
    return pl.pallas_call(
        functools.partial(kernel, sizes),
        out_shape=jax.ShapeDtypeStruct(adjoint_new.shape, F32),
        in_specs=[hbm, hbm, hbm, hbm, smem, smem],
        out_specs=pl.BlockSpec(memory_space=pltpu.VMEM),
        scratch_shapes=[
            pltpu.VMEM((fields, levels, cells), F32),
            pltpu.VMEM((n_lev, stencil, cells // n_lev), F32),
            pltpu.VMEM((stencil, cells), I32),
            pltpu.VMEM((blocks, slots), I32),
            pltpu.VMEM((LOW, blocks * slots), BF16),
            pltpu.VMEM((groups * (2 * rows + 16), LOW), BF16),
            pltpu.VMEM((stencil * groups, LOW), F32),
            pltpu.VMEM((blocks, rows, slots), F32),
            pltpu.VMEM((groups * 2 * rows, LOW), F32),
            pltpu.VMEM((blocks, rows + 8, slots), F32),
            pltpu.VMEM((blocks, rows + 8, slots), F32),
            pltpu.SemaphoreType.DMA((4,)),
            pltpu.SemaphoreType.DMA((n_lev - 1,)),
            pltpu.SemaphoreType.DMA((n_lev - 1,)),
            pltpu.SemaphoreType.DMA((blocks,)),
            pltpu.SemaphoreType.DMA((blocks,)),
        ],
        compiler_params=pltpu.CompilerParams(collective_id=0, has_side_effects=True),
    )(adjoint_new, weights, departure, send_point, block_count.reshape(-1), rotation.reshape(-1))


def solution(mesh):
    sizes = tuple(mesh.shape[a] for a in ("panel", "tile", "lev"))
    return jax.shard_map(
        functools.partial(body, sizes),
        mesh=mesh,
        in_specs=(
            P(None, "lev", ("panel", "tile")),
            P(None, ("panel", "tile", "lev")),
            P(None, ("panel", "tile")),
            P(None, ("panel", "tile")),
            P(None, ("panel", "tile")),
            P(None, ("panel", "tile")),
        ),
        out_specs=P(None, "lev", ("panel", "tile")),
        check_vma=False,
    )
```

time: 110 us -> 25.1 us (0.23)
  the two profiles are of different devices: /device:TPU:1 before, /device:TPU:8 now
where the time goes in v1:
time: 25.1 us; the launch traced here: 24.9 us
  Pallas kernels  23.2 us (92%)
  local copies, waits for them, and re-layouts  1.72 us (7%)
    pallas_call x1, Pallas kernels, body(): pl.pallas_call(functools.partial(kernel, sizes), out_shape=jax.ShapeDtype...  23.2 us
    unnamed x1, local copies, waits for them, and re-layouts  1.72 us

profile of v1, /device:TPU:8, one launch (start us, length us, event | category | flops | bytes accessed | tf_op | source)
XLA Modules:
  0.0 24.9 jit_solution(4048812794641773075)
XLA Ops:
  0.0 23.2 %shard_map.64 = f32[5,8,2048]{2,1,0:T(8,128)} custom-call(f32[5,8,2048]{2,1,0:T(8,128)} %x_hbm.1, f32[4,512]{1,0:T(4,128)} %w_hbm.1, s32[4,2048]{1,0:T(4,128)} %dep_hbm.1, s32[4,128]{1,0:T(4,128)} %sp_hbm.1, s32[4]{0:T(128)} %bitcast.2, s32[2]{0:T(128)} %bitcast.3), custom_call_target="tpu_custom_call" | custom-call | tf_op jit(solution)/shard_map/pallas_call | solution.py:297
  23.2 1.7 %copy.8 = f32[5,8,2048]{2,1,0:T(8,128)} copy(f32[5,8,2048]{2,1,0:T(8,128)} %shard_map.64) | data formatting | bytes 655360

commit v2 on v1

--- a/solution.py
+++ b/solution.py
@@ -43,9 +43,11 @@
     w_hbm,
     dep_hbm,
     sp_hbm,
+    count_hbm,
+    turn_hbm,
+    out_ref,
     count_ref,
     turn_ref,
-    out_ref,
     x,
     w,
     dep,
@@ -77,7 +79,16 @@
 
     loads = [
         pltpu.make_async_copy(src, dst, in_sem.at[i])
-        for i, (src, dst) in enumerate(((w_hbm, w.at[0]), (sp_hbm, sp), (dep_hbm, dep), (x_hbm, x)))
+        for i, (src, dst) in enumerate(
+            (
+                (w_hbm, w.at[0]),
+                (sp_hbm, sp),
+                (dep_hbm, dep),
+                (x_hbm, x),
+                (count_hbm, count_ref),
+                (turn_hbm, turn_ref),
+            )
+        )
     ]
     for load in loads:
         load.start()
@@ -102,26 +113,8 @@
     def _():
         greet({"tile": tile + 1})
 
-    loads[0].wait()
-    pl.semaphore_wait(barrier, n_lev + 1 + has_prev.astype(I32) + has_next.astype(I32))
-
-    w_copies = [
-        pltpu.make_async_remote_copy(
-            src_ref=w.at[0],
-            dst_ref=w.at[n_lev - d],
-            send_sem=w_send.at[d - 1],
-            recv_sem=w_recv.at[n_lev - d - 1],
-            device_id={"lev": lax.rem(lev + d, n_lev)},
-            device_id_type=MESH,
-        )
-        for d in range(1, n_lev)
-    ]
-    for copy in w_copies:
-        copy.start()
-
-    loads[1].wait()
-    loads[2].wait()
-    loads[3].wait()
+    for load in loads[1:]:
+        load.wait()
 
     point = [sp[j : j + 1, :] for j in range(blocks)]
     cell_high = [(p & (cells - 1)) >> shift_low for p in point]
@@ -162,6 +155,23 @@
                 jnp.where(own, total[2 * rows : 2 * rows + 8] * scale, 0.0), axis=0, keepdims=True
             )
             pay[j, rows : rows + 8, :] = jnp.broadcast_to(target, (8, slots))
+
+    loads[0].wait()
+    pl.semaphore_wait(barrier, n_lev + 1 + has_prev.astype(I32) + has_next.astype(I32))
+
+    w_copies = [
+        pltpu.make_async_remote_copy(
+            src_ref=w.at[0],
+            dst_ref=w.at[n_lev - d],
+            send_sem=w_send.at[d - 1],
+            recv_sem=w_recv.at[n_lev - d - 1],
+            device_id={"lev": lax.rem(lev + d, n_lev)},
+            device_id_type=MESH,
+        )
+        for d in range(1, n_lev)
+    ]
+    for copy in w_copies:
+        copy.start()
 
     def segment(d):
         first = lax.rem(lev + d, n_lev)
@@ -292,14 +302,16 @@
     rows = fields * levels
     groups = cells // LOW
     n_lev = sizes[2]
-    hbm = pl.BlockSpec(memory_space=pl.ANY)
-    smem = pl.BlockSpec(memory_space=pltpu.SMEM)
+    hbm = pl.BlockSpec(memory_space=pltpu.HBM)
+    args = (adjoint_new, weights, departure, send_point, block_count.reshape(-1), rotation.reshape(-1))
     return pl.pallas_call(
         functools.partial(kernel, sizes),
-        out_shape=jax.ShapeDtypeStruct(adjoint_new.shape, F32),
-        in_specs=[hbm, hbm, hbm, hbm, smem, smem],
+        out_shape=pltpu.VMEM(adjoint_new.shape, F32),
+        in_specs=[hbm] * len(args),
         out_specs=pl.BlockSpec(memory_space=pltpu.VMEM),
         scratch_shapes=[
+            pltpu.SMEM((blocks,), I32),
+            pltpu.SMEM((rotation.shape[0],), I32),
             pltpu.VMEM((fields, levels, cells), F32),
             pltpu.VMEM((n_lev, stencil, cells // n_lev), F32),
             pltpu.VMEM((stencil, cells), I32),
@@ -311,14 +323,16 @@
             pltpu.VMEM((groups * 2 * rows, LOW), F32),
             pltpu.VMEM((blocks, rows + 8, slots), F32),
             pltpu.VMEM((blocks, rows + 8, slots), F32),
-            pltpu.SemaphoreType.DMA((4,)),
+            pltpu.SemaphoreType.DMA((len(args),)),
             pltpu.SemaphoreType.DMA((n_lev - 1,)),
             pltpu.SemaphoreType.DMA((n_lev - 1,)),
             pltpu.SemaphoreType.DMA((blocks,)),
             pltpu.SemaphoreType.DMA((blocks,)),
         ],
-        compiler_params=pltpu.CompilerParams(collective_id=0, has_side_effects=True),
-    )(adjoint_new, weights, departure, send_point, block_count.reshape(-1), rotation.reshape(-1))
+        compiler_params=pltpu.CompilerParams(
+            collective_id=0, has_side_effects=True, vmem_limit_bytes=16 * 1024 * 1024
+        ),
+    )(*(pltpu.with_memory_space_constraint(a, pltpu.HBM) for a in args))
 
 
 def solution(mesh):

time: 25.1 us -> 22.7 us (0.904)
  Pallas kernels: 23.2 us -> 21.8 us
  local copies, waits for them, and re-layouts: 1.72 us -> 0.73 us
    pallas_call x1, Pallas kernels: 23.2 us -> 21.8 us  [body(): pl.pallas_call(functools.partial(kernel, sizes), out_shape=pltpu.VMEM(adj...]
    unnamed x1, local copies, waits for them, and re-layouts: 1.72 us -> 0.73 us
where the time goes in v2:
time: 22.7 us; the launch traced here: 22.6 us
  Pallas kernels  21.8 us (96%)
  local copies, waits for them, and re-layouts  0.73 us (3%)
    pallas_call x1, Pallas kernels, body(): pl.pallas_call(functools.partial(kernel, sizes), out_shape=pltpu.VMEM(adj...  21.8 us
    unnamed x1, local copies, waits for them, and re-layouts  0.73 us

profile of v2, /device:TPU:8, one launch (start us, length us, event | category | flops | bytes accessed | tf_op | source)
XLA Modules:
  0.0 22.6 jit_solution(12789149708312367133)
XLA Ops:
  0.0 21.8 %shard_map.64 = f32[5,8,2048]{2,1,0:T(8,128)S(1)} custom-call(f32[5,8,2048]{2,1,0:T(8,128)} %x_hbm.1, f32[4,512]{1,0:T(4,128)} %w_hbm.1, s32[4,2048]{1,0:T(4,128)} %dep_hbm.1, s32[4,128]{1,0:T(4,128)} %sp_hbm.1, s32[4]{0:T(128)} %bitcast.2, s32[2]{0:T(128)} %bitcast.3), custom_call_target="tpu_custom_call" | custom-call | tf_op jit(solution)/shard_map/pallas_call | solution.py:307
  21.8 0.7 %copy.8 = f32[5,8,2048]{2,1,0:T(8,128)} copy(f32[5,8,2048]{2,1,0:T(8,128)S(1)} %shard_map.64) | data formatting | bytes 655360

commit v3 on v2

v3 whole, which is shorter than its diff:
```python
import functools

import jax
import jax.numpy as jnp
from jax import lax
from jax.experimental import pallas as pl
from jax.experimental.pallas import tpu as pltpu
from jax.sharding import PartitionSpec as P

MESH = pl.DeviceIdType.MESH
LOW = 256
F32, BF16, I32 = jnp.float32, jnp.bfloat16, jnp.int32


def split_rows(value):
    high = value.astype(BF16).astype(F32)
    return jnp.concatenate([high, value - high], axis=0).astype(BF16)


def one_hot(low, columns):
    rows = lax.broadcasted_iota(I32, (LOW, columns), 0)
    return jnp.where(rows == low, 1.0, 0.0).astype(BF16)


def times_transposed(lhs, rhs):
    return lax.dot_general(lhs, rhs, (((1,), (1,)), ((), ())), preferred_element_type=F32)


def spread(value, target_high, target_low, groups):
    parts = split_rows(value)
    copies = parts.shape[0] // 16
    high = jnp.broadcast_to(target_high, (16, LOW))
    lhs = []
    for g in range(groups):
        mask = jnp.where(high == g, 1.0, 0.0).astype(BF16)
        lhs.append(parts * jnp.concatenate([mask] * copies, axis=0))
    return times_transposed(jnp.concatenate(lhs, axis=0), one_hot(target_low, LOW))


def kernel(
    sizes,
    x_hbm,
    w_hbm,
    dep_hbm,
    sp_hbm,
    count_hbm,
    turn_hbm,
    out_ref,
    count_ref,
    turn_ref,
    x,
    w,
    relay,
    dep,
    sp,
    hot,
    glhs,
    sent,
    acc,
    pay,
    recv,
    extra,
    in_sem,
    w_send,
    w_recv,
    r_recv,
    z_send,
    z_recv,
    p_send,
    p_recv,
    e_send,
    e_recv,
):
    n_panel, n_tile, n_lev = sizes
    fields, levels, cells = x.shape
    stencil = dep.shape[0]
    blocks, slots = sp.shape
    rows = fields * levels
    groups = cells // LOW
    share = cells // n_lev
    per_lev = share // LOW
    panel, tile, lev = (lax.axis_index(a) for a in ("panel", "tile", "lev"))
    shift_cell = cells.bit_length() - 1
    shift_low = LOW.bit_length() - 1
    at_slot = rows + 8

    odd = lax.rem(tile, 2) == 1
    even = jnp.logical_not(odd)
    first = lev == 0
    lone = jnp.logical_and(even, first)
    helper = jnp.logical_and(odd, first)
    feeder = jnp.logical_and(even, jnp.logical_not(first))
    second = jnp.logical_and(even, lev == 1)
    other = jnp.logical_and(odd, jnp.logical_not(first))
    has_prev, has_next = tile > 0, tile < n_tile - 1
    yes = tile >= 0
    next_panel, prev_panel = lax.rem(panel + 1, n_panel), lax.rem(panel + n_panel - 1, n_panel)
    prev_tile, next_tile = jnp.maximum(tile - 1, 0), jnp.minimum(tile + 1, n_tile - 1)
    toward = [{"tile": prev_tile}, {"tile": next_tile}, {"panel": prev_panel}, {"panel": next_panel}]
    sends_to = [has_prev, has_next, yes, yes]
    comes_from = [{"tile": next_tile}, {"tile": prev_tile}, {"panel": next_panel}, {"panel": prev_panel}]
    hears = [has_next, has_prev, yes, yes]
    from_even = [odd, odd, even, even]

    loads = [
        pltpu.make_async_copy(src, dst, in_sem.at[i])
        for i, (src, dst) in enumerate(
            (
                (sp_hbm, sp),
                (w_hbm, w.at[lev]),
                (count_hbm, count_ref),
                (turn_hbm, turn_ref),
                (dep_hbm, dep),
                (x_hbm, x),
            )
        )
    ]
    for load in loads:
        load.start()

    barrier = pltpu.get_barrier_semaphore()

    def greet(device):
        pl.semaphore_signal(barrier, inc=1, device_id=device, device_id_type=MESH)

    @pl.when(lone)
    def _():
        greet({"tile": next_tile})

    @pl.when(jnp.logical_not(lone))
    def _():
        for d in range(1, n_lev):
            greet({"lev": lax.rem(lev + d, n_lev)})
        for j in range(blocks):

            @pl.when(hears[j])
            def _(j=j):
                greet(comes_from[j])

                @pl.when(from_even[j])
                def _():
                    greet({**comes_from[j], "lev": jnp.where(first, 1, 0)})

    @pl.when(helper)
    def _():
        for t in range(1, n_lev):
            greet({"tile": prev_tile, "lev": t})
        for p in (prev_panel, next_panel):
            for t in range(2):
                greet({"panel": p, "tile": prev_tile, "lev": t})

        @pl.when(tile > 1)
        def _():
            greet({"tile": tile - 2})

    acc[...] = jnp.zeros_like(acc)

    sent_blocks = 2 + has_prev.astype(I32) + has_next.astype(I32)
    more = jnp.where(lone, n_lev - 1, 0) + jnp.where(second, 1, 0)

    def weight_copy(d, dst, sem, device):
        return pltpu.make_async_remote_copy(
            src_ref=w.at[lev],
            dst_ref=dst.at[lev],
            send_sem=w_send.at[d - 1],
            recv_sem=sem.at[lev],
            device_id=device,
            device_id_type=MESH,
        )

    def enter():
        pl.semaphore_wait(barrier, n_lev - 1 + sent_blocks * (1 + more))
        for d in range(1, n_lev):
            indirect = jnp.logical_and(even, lev == n_lev - d)

            @pl.when(indirect)
            def _(d=d):
                weight_copy(d, relay, r_recv, {"tile": next_tile, "lev": 0}).start()

            @pl.when(jnp.logical_not(indirect))
            def _(d=d):
                weight_copy(d, w, w_recv, {"lev": lax.rem(lev + d, n_lev)}).start()

    for load in loads[:2]:
        load.wait()

    @pl.when(lone)
    def _():
        enter()

    for load in loads[2:4]:
        load.wait()

    point = [sp[j : j + 1, :] for j in range(blocks)]
    cell_high = [(p & (cells - 1)) >> shift_low for p in point]
    stencil_of = [p >> shift_cell for p in point]
    lane = lax.broadcasted_iota(I32, (1, slots), 1)
    live = [lane < count_ref[j] for j in range(blocks)]
    for j in range(blocks):
        hot[:, j * slots : (j + 1) * slots] = one_hot(point[j] & (LOW - 1), slots)

    def slot_weights(parts):
        lhs = []
        for t in parts:
            for i in range(per_lev):
                w4 = w[t, :, i * LOW : (i + 1) * LOW]
                b1 = w4.astype(BF16).astype(F32)
                b2 = (w4 - b1).astype(BF16).astype(F32)
                lhs.append(
                    jnp.concatenate([b1, b2, w4 - b1 - b2, jnp.zeros_like(w4)], axis=0).astype(BF16)
                )
        found = jnp.dot(jnp.concatenate(lhs, axis=0), hot[...], preferred_element_type=F32)
        row16 = lax.broadcasted_iota(I32, (16, slots), 0)
        result = []
        for j in range(blocks):
            total = jnp.zeros((16, slots), F32)
            for n, t in enumerate(parts):
                for i in range(per_lev):
                    r = n * per_lev + i
                    piece = found[r * 16 : (r + 1) * 16, j * slots : (j + 1) * slots]
                    total = total + jnp.where(cell_high[j] == t * per_lev + i, piece, 0.0)
            own = (row16 & (stencil - 1)) == stencil_of[j]
            weight = jnp.sum(jnp.where(own, total, 0.0), axis=0, keepdims=True)
            result.append(jnp.where(live[j], weight, 0.0))
        return result

    for j, weight in enumerate(slot_weights([lev])):
        pay[j, at_slot:, :] = jnp.broadcast_to(weight, (8, slots))

    def ahead(j, moved):
        if j >= 2:
            return {**toward[j], "tile": tile + moved}
        return {"tile": toward[j]["tile"] + moved}

    def block_copy(j):
        moved = jnp.where(helper, 1, 0) if j == 1 else (jnp.where(lone, 1, 0) if j >= 2 else 0)
        return pltpu.make_async_remote_copy(
            src_ref=pay.at[j],
            dst_ref=recv.at[j + blocks * moved],
            send_sem=p_send.at[j],
            recv_sem=p_recv.at[j + blocks * moved],
            device_id=ahead(j, moved),
            device_id_type=MESH,
        )

    def extra_copy(j, n, level):
        moved = jnp.where(second, 1, 0) if level == 0 and j >= 2 else 0
        return pltpu.make_async_remote_copy(
            src_ref=pay.at[j, pl.ds(at_slot, 8)],
            dst_ref=extra.at[j + blocks * moved],
            send_sem=e_send.at[j, n],
            recv_sem=e_recv.at[j + blocks * moved],
            device_id={**ahead(j, moved), "lev": level},
            device_id_type=MESH,
        )

    def send_blocks():
        for j in (1, 0, 2, 3):

            @pl.when(sends_to[j])
            def _(j=j):
                block_copy(j).start()

    @pl.when(lone)
    def _():
        for t in range(1, n_lev):
            for j in (1, 0, 2, 3):

                @pl.when(sends_to[j])
                def _(j=j, t=t):
                    extra_copy(j, t - 1, t).start()

    for load in loads[4:]:
        load.wait()

    height = 2 * rows + 16
    for g in range(groups):
        part = x[:, :, g * LOW : (g + 1) * LOW].reshape(rows, LOW)
        d4 = dep[:, g * LOW : (g + 1) * LOW]
        d8 = jnp.concatenate([d4 >> shift_low, d4 & (LOW - 1)], axis=0).astype(F32)
        d16 = jnp.concatenate([d8, jnp.zeros((8, LOW), F32)], axis=0).astype(BF16)
        glhs[g * height : g * height + 2 * rows, :] = split_rows(part)
        glhs[g * height + 2 * rows : (g + 1) * height, :] = d16
    row8 = lax.broadcasted_iota(I32, (8, slots), 0)
    for n in range(blocks * slots // LOW):
        found = jnp.dot(glhs[...], hot[:, n * LOW : (n + 1) * LOW], preferred_element_type=F32)
        for i in range(LOW // slots):
            j = n * (LOW // slots) + i
            total = jnp.zeros((height, slots), F32)
            for g in range(groups):
                piece = found[g * height : (g + 1) * height, i * slots : (i + 1) * slots]
                total = total + jnp.where(cell_high[j] == g, piece, 0.0)
            value = total[:rows] + total[rows : 2 * rows]
            if j >= 2:
                code = turn_ref[j - 2]
                cosine = jnp.where(code == 0, 1.0, 0.0) - jnp.where(code == 2, 1.0, 0.0)
                sine = jnp.where(code == 1, 1.0, 0.0) - jnp.where(code == 3, 1.0, 0.0)
                zonal, merid = value[:levels], value[levels : 2 * levels]
                value = jnp.concatenate(
                    [
                        cosine * zonal + sine * merid,
                        cosine * merid - sine * zonal,
                        value[2 * levels :],
                    ],
                    axis=0,
                )
            scale = jnp.where(row8 < stencil, float(LOW), 1.0)
            own = (row8 & (stencil - 1)) == stencil_of[j]
            target = jnp.sum(
                jnp.where(own, total[2 * rows : 2 * rows + 8] * scale, 0.0), axis=0, keepdims=True
            )
            pay[j, 0:rows, :] = value
            pay[j, rows:at_slot, :] = jnp.broadcast_to(target, (8, slots))

    @pl.when(lone)
    def _():
        send_blocks()

    number = lax.broadcasted_iota(I32, (stencil * groups, slots), 0)
    marks = [
        jnp.where((number == (point[j] >> shift_low)) & live[j], 1.0, 0.0).astype(BF16)
        for j in range(blocks)
    ]
    sent[...] = times_transposed(jnp.concatenate(marks, axis=1), hot[...])

    def segment(t):
        result = None
        for i in range(per_lev):
            at = pl.ds(pl.multiple_of(t * share + i * LOW, LOW), LOW)
            part = x[:, :, at].reshape(rows, LOW)
            for k in range(stencil):
                weight = w[t, k : k + 1, i * LOW : (i + 1) * LOW]
                landing = dep[k : k + 1, at]
                gone = sent[pl.ds(k * groups + t * per_lev + i, 1), :]
                high = jnp.where(gone > 0.5, groups, landing >> shift_low)
                term = spread(part * weight, high, landing & (LOW - 1), groups)
                result = term if result is None else result + term
        return result

    order = [
        lev,
        jnp.where(first, 1, 1 + lax.rem(lev, 3)),
        jnp.where(first, 2, 1 + lax.rem(lev + 1, 3)),
        jnp.where(first, 3, 0),
    ]

    def arrival(buffer, sem, t):
        return pltpu.make_async_remote_copy(
            src_ref=buffer.at[t],
            dst_ref=buffer.at[t],
            send_sem=w_send.at[0],
            recv_sem=sem.at[t],
            device_id={"panel": next_panel},
            device_id_type=MESH,
        )

    def add_weights(parts):
        weights = slot_weights(parts)
        for j in range(blocks):
            pay[j, at_slot:, :] += jnp.broadcast_to(weights[j], (8, slots))
        send_blocks()

    def to_lone(src, dst, send_sem, recv_sem):
        return pltpu.make_async_remote_copy(
            src_ref=src,
            dst_ref=dst,
            send_sem=send_sem,
            recv_sem=recv_sem,
            device_id={"tile": prev_tile},
            device_id_type=MESH,
        )

    others = pl.ds(1, n_lev - 1)
    relay_copy = to_lone(relay.at[others], w.at[others], z_send.at[0], z_recv)
    passed_on = [
        (j, to_lone(recv.at[blocks + j], recv.at[j], z_send.at[j], p_recv.at[j]))
        for j in range(1, blocks)
    ]
    passed_on_extra = [
        (j, to_lone(extra.at[blocks + j], extra.at[j], z_send.at[j + 2], e_recv.at[j]))
        for j in (2, 3)
    ]

    def both(*conditions):
        return functools.reduce(jnp.logical_and, conditions)

    def step(i, carry):
        @pl.when(i == jnp.where(helper, 2, jnp.where(other, 1, jnp.where(feeder, 0, -1))))
        def _():
            enter()

        when = (
            jnp.where(lone, -1, 1),
            jnp.where(lone, -1, jnp.where(feeder, 1, 2)),
            jnp.where(lone, -1, jnp.where(helper, 2, jnp.where(other, 3, 4))),
        )
        for n in range(3):

            @pl.when(i == when[n])
            def _(n=n):
                arrival(w, w_recv, order[n + 1]).wait_recv()

        @pl.when(both(odd, i == when[2]))
        def _():
            add_weights(order[1:])

        @pl.when(both(feeder, i == 1))
        def _():
            add_weights(order[1:3])

            @pl.when(second)
            def _():
                for j in range(blocks):

                    @pl.when(sends_to[j])
                    def _(j=j):
                        extra_copy(j, 0, 0).start()

        @pl.when(both(helper, i == 2))
        def _():
            for t in range(1, n_lev):
                arrival(relay, r_recv, t).wait_recv()
            relay_copy.start()

        @pl.when(both(lone, i == 1))
        def _():
            relay_copy.wait_recv()

        @pl.when(both(helper, i == 4))
        def _():
            for j, copy in passed_on:

                @pl.when(tile > 1 if j == 1 else yes)
                def _(j=j, copy=copy):
                    arrival(recv, p_recv, blocks + j).wait_recv()
                    copy.start()

            for j, copy in passed_on_extra:
                arrival(extra, e_recv, blocks + j).wait_recv()
                copy.start()

        arriving = i == jnp.where(feeder, 3, 4)

        @pl.when(jnp.logical_not(arriving))
        def _():
            k = jnp.minimum(i, 3)
            t = jnp.where(
                k == 0, order[0], jnp.where(k == 1, order[1], jnp.where(k == 2, order[2], order[3]))
            )
            acc[...] += segment(t)

        @pl.when(arriving)
        def _():
            for j in range(blocks):

                @pl.when(hears[j])
                def _(j=j):
                    arrival(recv, p_recv, j).wait_recv()

                @pl.when(jnp.logical_not(hears[j]))
                def _(j=j):
                    recv[j] = jnp.zeros_like(recv[j])

                also = jnp.logical_and(hears[j], from_even[j])

                @pl.when(also)
                def _(j=j):
                    arrival(extra, e_recv, j).wait_recv()

                @pl.when(jnp.logical_not(also))
                def _(j=j):
                    extra[j] = jnp.zeros_like(extra[j])

            result = acc[...]
            for pair in ((0, 2), (1, 3)):
                value = jnp.concatenate(
                    [
                        recv[j, 0:rows] * (recv[j, at_slot : at_slot + 1] + extra[j, 0:1])
                        for j in pair
                    ],
                    axis=1,
                )
                landing = jnp.concatenate([recv[j, rows : rows + 1] for j in pair], axis=1).astype(I32)
                result = result + spread(value, landing >> shift_low, landing & (LOW - 1), groups)
            acc[...] = result

        return carry

    lax.fori_loop(0, 5, step, 0)

    result = acc
    for g in range(groups):
        top = g * 2 * rows
        out_ref[:, :, g * LOW : (g + 1) * LOW] = (
            result[top : top + rows, :] + result[top + rows : top + 2 * rows, :]
        ).reshape(fields, levels, LOW)

    for d in range(1, n_lev):
        weight_copy(d, w, w_recv, {"lev": lax.rem(lev + d, n_lev)}).wait_send()
    for j in range(blocks):

        @pl.when(sends_to[j])
        def _(j=j):
            block_copy(j).wait_send()

            @pl.when(lone)
            def _():
                for t in range(1, n_lev):
                    extra_copy(j, t - 1, t).wait_send()

            @pl.when(second)
            def _():
                extra_copy(j, 0, 0).wait_send()

    @pl.when(helper)
    def _():
        relay_copy.wait_send()
        for j, copy in passed_on:

            @pl.when(tile > 1 if j == 1 else yes)
            def _(copy=copy):
                copy.wait_send()

        for j, copy in passed_on_extra:
            copy.wait_send()


def body(sizes, adjoint_new, weights, departure, send_point, block_count, rotation):
    fields, levels, cells = adjoint_new.shape
    stencil = departure.shape[0]
    blocks, slots = send_point.shape
    rows = fields * levels
    groups = cells // LOW
    n_lev = sizes[2]
    hbm = pl.BlockSpec(memory_space=pltpu.HBM)
    args = (adjoint_new, weights, departure, send_point, block_count.reshape(-1), rotation.reshape(-1))
    return pl.pallas_call(
        functools.partial(kernel, sizes),
        out_shape=pltpu.VMEM(adjoint_new.shape, F32),
        in_specs=[hbm] * len(args),
        out_specs=pl.BlockSpec(memory_space=pltpu.VMEM),
        scratch_shapes=[
            pltpu.SMEM((blocks,), I32),
            pltpu.SMEM((rotation.shape[0],), I32),
            pltpu.VMEM((fields, levels, cells), F32),
            pltpu.VMEM((n_lev, stencil, cells // n_lev), F32),
            pltpu.VMEM((n_lev, stencil, cells // n_lev), F32),
            pltpu.VMEM((stencil, cells), I32),
            pltpu.VMEM((blocks, slots), I32),
            pltpu.VMEM((LOW, blocks * slots), BF16),
            pltpu.VMEM((groups * (2 * rows + 16), LOW), BF16),
            pltpu.VMEM((stencil * groups, LOW), F32),
            pltpu.VMEM((groups * 2 * rows, LOW), F32),
            pltpu.VMEM((blocks, rows + 16, slots), F32),
            pltpu.VMEM((2 * blocks, rows + 16, slots), F32),
            pltpu.VMEM((2 * blocks, 8, slots), F32),
            pltpu.SemaphoreType.DMA((len(args),)),
            pltpu.SemaphoreType.DMA((n_lev - 1,)),
            pltpu.SemaphoreType.DMA((n_lev,)),
            pltpu.SemaphoreType.DMA((n_lev,)),
            pltpu.SemaphoreType.DMA((blocks + 2,)),
            pltpu.SemaphoreType.DMA,
            pltpu.SemaphoreType.DMA((blocks,)),
            pltpu.SemaphoreType.DMA((2 * blocks,)),
            pltpu.SemaphoreType.DMA((blocks, n_lev - 1)),
            pltpu.SemaphoreType.DMA((2 * blocks,)),
        ],
        compiler_params=pltpu.CompilerParams(
            collective_id=0, has_side_effects=True, vmem_limit_bytes=16 * 1024 * 1024
        ),
    )(*(pltpu.with_memory_space_constraint(a, pltpu.HBM) for a in args))


def solution(mesh):
    sizes = tuple(mesh.shape[a] for a in ("panel", "tile", "lev"))
    return jax.shard_map(
        functools.partial(body, sizes),
        mesh=mesh,
        in_specs=(
            P(None, "lev", ("panel", "tile")),
            P(None, ("panel", "tile", "lev")),
            P(None, ("panel", "tile")),
            P(None, ("panel", "tile")),
            P(None, ("panel", "tile")),
            P(None, ("panel", "tile")),
        ),
        out_specs=P(None, "lev", ("panel", "tile")),
        check_vma=False,
    )
```

time: 22.7 us -> 19.5 us (0.86)
  Pallas kernels: 21.8 us -> 18.6 us
    pallas_call x1, Pallas kernels: 21.8 us -> 18.6 us  [body(): pl.pallas_call(functools.partial(kernel, sizes), out_shape=pltpu.VMEM(adj...]
where the time goes in v3:
time: 19.5 us; the launch traced here: 19.4 us
  Pallas kernels  18.6 us (95%)
  local copies, waits for them, and re-layouts  0.73 us (4%)
    pallas_call x1, Pallas kernels, body(): pl.pallas_call(functools.partial(kernel, sizes), out_shape=pltpu.VMEM(adj...  18.6 us
    unnamed x1, local copies, waits for them, and re-layouts  0.73 us

profile of v3, /device:TPU:8, one launch (start us, length us, event | category | flops | bytes accessed | tf_op | source)
XLA Modules:
  0.0 19.4 jit_solution(4633839950312457025)
XLA Ops:
  0.0 18.6 %shard_map.64 = f32[5,8,2048]{2,1,0:T(8,128)S(1)} custom-call(f32[5,8,2048]{2,1,0:T(8,128)} %x_hbm.1, f32[4,512]{1,0:T(4,128)} %w_hbm.1, s32[4,2048]{1,0:T(4,128)} %dep_hbm.1, s32[4,128]{1,0:T(4,128)} %sp_hbm.1, s32[4]{0:T(128)} %bitcast.2, s32[2]{0:T(128)} %bitcast.3), custom_call_target="tpu_custom_call" | custom-call | tf_op jit(solution)/shard_map/pallas_call | solution.py:537
  18.6 0.7 %copy.8 = f32[5,8,2048]{2,1,0:T(8,128)} copy(f32[5,8,2048]{2,1,0:T(8,128)S(1)} %shard_map.64) | data formatting | bytes 655360

commit v4 on v3

--- a/solution.py
+++ b/solution.py
@@ -58,18 +58,15 @@
     sent,
     acc,
     pay,
-    recv,
-    extra,
+    inbox,
+    w_recv,
+    r_recv,
+    p_recv,
     in_sem,
     w_send,
-    w_recv,
-    r_recv,
+    p_send,
+    e_send,
     z_send,
-    z_recv,
-    p_send,
-    p_recv,
-    e_send,
-    e_recv,
 ):
     n_panel, n_tile, n_lev = sizes
     fields, levels, cells = x.shape
@@ -83,6 +80,8 @@
     shift_cell = cells.bit_length() - 1
     shift_low = LOW.bit_length() - 1
     at_slot = rows + 8
+    size = rows + 16
+    extras = blocks * size
 
     odd = lax.rem(tile, 2) == 1
     even = jnp.logical_not(odd)
@@ -93,6 +92,7 @@
     second = jnp.logical_and(even, lev == 1)
     other = jnp.logical_and(odd, jnp.logical_not(first))
     has_prev, has_next = tile > 0, tile < n_tile - 1
+    whole = jnp.logical_and(has_prev, has_next)
     yes = tile >= 0
     next_panel, prev_panel = lax.rem(panel + 1, n_panel), lax.rem(panel + n_panel - 1, n_panel)
     prev_tile, next_tile = jnp.maximum(tile - 1, 0), jnp.minimum(tile + 1, n_tile - 1)
@@ -154,6 +154,12 @@
             greet({"tile": tile - 2})
 
     acc[...] = jnp.zeros_like(acc)
+    for j in range(2):
+
+        @pl.when(jnp.logical_not(hears[j]))
+        def _(j=j):
+            inbox[j * size : (j + 1) * size, :] = jnp.zeros((size, slots), F32)
+
 
     sent_blocks = 2 + has_prev.astype(I32) + has_next.astype(I32)
     more = jnp.where(lone, n_lev - 1, 0) + jnp.where(second, 1, 0)
@@ -162,8 +168,8 @@
         return pltpu.make_async_remote_copy(
             src_ref=w.at[lev],
             dst_ref=dst.at[lev],
-            send_sem=w_send.at[d - 1],
-            recv_sem=sem.at[lev],
+            send_sem=w_send,
+            recv_sem=sem,
             device_id=device,
             device_id_type=MESH,
         )
@@ -179,7 +185,7 @@
 
             @pl.when(jnp.logical_not(indirect))
             def _(d=d):
-                weight_copy(d, w, w_recv, {"lev": lax.rem(lev + d, n_lev)}).start()
+                weight_copy(d, w, w_recv.at[lev], {"lev": lax.rem(lev + d, n_lev)}).start()
 
     for load in loads[:2]:
         load.wait()
@@ -224,9 +230,6 @@
             result.append(jnp.where(live[j], weight, 0.0))
         return result
 
-    for j, weight in enumerate(slot_weights([lev])):
-        pay[j, at_slot:, :] = jnp.broadcast_to(weight, (8, slots))
-
     def ahead(j, moved):
         if j >= 2:
             return {**toward[j], "tile": tile + moved}
@@ -234,22 +237,23 @@
 
     def block_copy(j):
         moved = jnp.where(helper, 1, 0) if j == 1 else (jnp.where(lone, 1, 0) if j >= 2 else 0)
+        at = j * size if j == 0 else pl.multiple_of(j * size + moved * (blocks * (size + 8) - size), 8)
         return pltpu.make_async_remote_copy(
             src_ref=pay.at[j],
-            dst_ref=recv.at[j + blocks * moved],
-            send_sem=p_send.at[j],
-            recv_sem=p_recv.at[j + blocks * moved],
+            dst_ref=inbox.at[pl.ds(at, size)],
+            send_sem=p_send,
+            recv_sem=p_recv.at[moved],
             device_id=ahead(j, moved),
             device_id_type=MESH,
         )
 
-    def extra_copy(j, n, level):
+    def extra_copy(j, level):
         moved = jnp.where(second, 1, 0) if level == 0 and j >= 2 else 0
         return pltpu.make_async_remote_copy(
             src_ref=pay.at[j, pl.ds(at_slot, 8)],
-            dst_ref=extra.at[j + blocks * moved],
-            send_sem=e_send.at[j, n],
-            recv_sem=e_recv.at[j + blocks * moved],
+            dst_ref=inbox.at[pl.ds(extras + 8 * j, 8)],
+            send_sem=e_send,
+            recv_sem=p_recv.at[moved],
             device_id={**ahead(j, moved), "lev": level},
             device_id_type=MESH,
         )
@@ -260,6 +264,9 @@
             @pl.when(sends_to[j])
             def _(j=j):
                 block_copy(j).start()
+
+    for j, weight in enumerate(slot_weights([lev])):
+        pay[j, at_slot:, :] = jnp.broadcast_to(weight, (8, slots))
 
     @pl.when(lone)
     def _():
@@ -268,7 +275,7 @@
 
                 @pl.when(sends_to[j])
                 def _(j=j, t=t):
-                    extra_copy(j, t - 1, t).start()
+                    extra_copy(j, t).start()
 
     for load in loads[4:]:
         load.wait()
@@ -344,15 +351,8 @@
         jnp.where(first, 3, 0),
     ]
 
-    def arrival(buffer, sem, t):
-        return pltpu.make_async_remote_copy(
-            src_ref=buffer.at[t],
-            dst_ref=buffer.at[t],
-            send_sem=w_send.at[0],
-            recv_sem=sem.at[t],
-            device_id={"panel": next_panel},
-            device_id_type=MESH,
-        )
+    def await_bytes(ref, sem):
+        pltpu.make_async_copy(ref, ref, sem).wait()
 
     def add_weights(parts):
         weights = slot_weights(parts)
@@ -371,34 +371,37 @@
         )
 
     others = pl.ds(1, n_lev - 1)
-    relay_copy = to_lone(relay.at[others], w.at[others], z_send.at[0], z_recv)
-    passed_on = [
-        (j, to_lone(recv.at[blocks + j], recv.at[j], z_send.at[j], p_recv.at[j]))
-        for j in range(1, blocks)
-    ]
-    passed_on_extra = [
-        (j, to_lone(extra.at[blocks + j], extra.at[j], z_send.at[j + 2], e_recv.at[j]))
-        for j in (2, 3)
-    ]
+    relay_copy = to_lone(relay.at[others], w.at[others], z_send.at[0], w_recv.at[0])
+    aside = blocks * (size + 8)
+    last_two = pl.ds(2 * size, 2 * size)
+    last_extras = pl.ds(extras + 16, 16)
+    pass_one = to_lone(inbox.at[pl.ds(aside, size)], inbox.at[pl.ds(size, size)], z_send.at[1], p_recv.at[0])
+    pass_two = to_lone(
+        inbox.at[pl.ds(aside + size, 2 * size)], inbox.at[last_two], z_send.at[1], p_recv.at[0]
+    )
+    pass_extras = to_lone(inbox.at[last_extras], inbox.at[last_extras], z_send.at[1], p_recv.at[0])
+    passed = 3 * size + 16, 2 * size + 16
 
     def both(*conditions):
         return functools.reduce(jnp.logical_and, conditions)
 
+    soon = both(feeder, lax.rem(panel, 2) == 0)
+
     def step(i, carry):
-        @pl.when(i == jnp.where(helper, 2, jnp.where(other, 1, jnp.where(feeder, 0, -1))))
+        @pl.when(i == jnp.where(helper, 3, jnp.where(other, 1, jnp.where(feeder, 0, -1))))
         def _():
             enter()
 
         when = (
             jnp.where(lone, -1, 1),
             jnp.where(lone, -1, jnp.where(feeder, 1, 2)),
-            jnp.where(lone, -1, jnp.where(helper, 2, jnp.where(other, 3, 4))),
+            jnp.where(lone, -1, jnp.where(soon, 4, 3)),
         )
         for n in range(3):
 
             @pl.when(i == when[n])
             def _(n=n):
-                arrival(w, w_recv, order[n + 1]).wait_recv()
+                await_bytes(w.at[order[n + 1]], w_recv.at[order[n + 1]])
 
         @pl.when(both(odd, i == when[2]))
         def _():
@@ -414,32 +417,32 @@
 
                     @pl.when(sends_to[j])
                     def _(j=j):
-                        extra_copy(j, 0, 0).start()
-
-        @pl.when(both(helper, i == 2))
-        def _():
-            for t in range(1, n_lev):
-                arrival(relay, r_recv, t).wait_recv()
+                        extra_copy(j, 0).start()
+
+        @pl.when(both(helper, i == 3))
+        def _():
+            await_bytes(relay.at[others], r_recv)
             relay_copy.start()
 
         @pl.when(both(lone, i == 1))
         def _():
-            relay_copy.wait_recv()
+            await_bytes(w.at[others], w_recv.at[0])
+
+        @pl.when(both(helper, i == 4, tile > 1))
+        def _():
+            await_bytes(inbox.at[pl.ds(0, passed[0])], p_recv.at[1])
+            pass_one.start()
+
+        @pl.when(both(helper, i == 4, tile == 1))
+        def _():
+            await_bytes(inbox.at[pl.ds(0, passed[1])], p_recv.at[1])
 
         @pl.when(both(helper, i == 4))
         def _():
-            for j, copy in passed_on:
-
-                @pl.when(tile > 1 if j == 1 else yes)
-                def _(j=j, copy=copy):
-                    arrival(recv, p_recv, blocks + j).wait_recv()
-                    copy.start()
-
-            for j, copy in passed_on_extra:
-                arrival(extra, e_recv, blocks + j).wait_recv()
-                copy.start()
-
-        arriving = i == jnp.where(feeder, 3, 4)
+            pass_two.start()
+            pass_extras.start()
+
+        arriving = i == jnp.where(soon, 3, 4)
 
         @pl.when(jnp.logical_not(arriving))
         def _():
@@ -451,36 +454,54 @@
 
         @pl.when(arriving)
         def _():
+            await_bytes(w.at[others], w_send)
+            for n, edge in ((blocks, whole), (blocks - 1, jnp.logical_not(whole))):
+
+                @pl.when(edge)
+                def _(n=n):
+                    await_bytes(pay.at[pl.ds(0, n)], p_send)
+
+                for role, times in ((lone, n_lev - 1), (second, 1)):
+
+                    @pl.when(both(role, edge))
+                    def _(n=n, times=times):
+                        await_bytes(inbox.at[pl.ds(0, 8 * n * times)], e_send)
+
+            @pl.when(helper)
+            def _():
+                await_bytes(relay.at[others], z_send.at[0])
+
+            for edge, n, m in (
+                (whole, blocks, 2),
+                (jnp.logical_not(has_prev), blocks - 1, 2),
+                (jnp.logical_not(has_next), blocks - 1, 1),
+            ):
+
+                @pl.when(edge)
+                def _(n=n, m=m):
+                    await_bytes(inbox.at[pl.ds(0, n * size + 8 * m)], p_recv.at[0])
+
             for j in range(blocks):
 
-                @pl.when(hears[j])
+                @pl.when(jnp.logical_and(hears[j], from_even[j]))
                 def _(j=j):
-                    arrival(recv, p_recv, j).wait_recv()
-
-                @pl.when(jnp.logical_not(hears[j]))
-                def _(j=j):
-                    recv[j] = jnp.zeros_like(recv[j])
-
-                also = jnp.logical_and(hears[j], from_even[j])
-
-                @pl.when(also)
-                def _(j=j):
-                    arrival(extra, e_recv, j).wait_recv()
-
-                @pl.when(jnp.logical_not(also))
-                def _(j=j):
-                    extra[j] = jnp.zeros_like(extra[j])
+                    inbox[j * size + at_slot : (j + 1) * size, :] += inbox[
+                        extras + 8 * j : extras + 8 * (j + 1), :
+                    ]
 
             result = acc[...]
             for pair in ((0, 2), (1, 3)):
                 value = jnp.concatenate(
                     [
-                        recv[j, 0:rows] * (recv[j, at_slot : at_slot + 1] + extra[j, 0:1])
+                        inbox[j * size : j * size + rows, :]
+                        * inbox[j * size + at_slot : j * size + at_slot + 1, :]
                         for j in pair
                     ],
                     axis=1,
                 )
-                landing = jnp.concatenate([recv[j, rows : rows + 1] for j in pair], axis=1).astype(I32)
+                landing = jnp.concatenate(
+                    [inbox[j * size + rows : j * size + rows + 1, :] for j in pair], axis=1
+                ).astype(I32)
                 result = result + spread(value, landing >> shift_low, landing & (LOW - 1), groups)
             acc[...] = result
 
@@ -495,34 +516,16 @@
             result[top : top + rows, :] + result[top + rows : top + 2 * rows, :]
         ).reshape(fields, levels, LOW)
 
-    for d in range(1, n_lev):
-        weight_copy(d, w, w_recv, {"lev": lax.rem(lev + d, n_lev)}).wait_send()
-    for j in range(blocks):
-
-        @pl.when(sends_to[j])
-        def _(j=j):
-            block_copy(j).wait_send()
-
-            @pl.when(lone)
-            def _():
-                for t in range(1, n_lev):
-                    extra_copy(j, t - 1, t).wait_send()
-
-            @pl.when(second)
-            def _():
-                extra_copy(j, 0, 0).wait_send()
-
-    @pl.when(helper)
-    def _():
-        relay_copy.wait_send()
-        for j, copy in passed_on:
-
-            @pl.when(tile > 1 if j == 1 else yes)
-            def _(copy=copy):
-                copy.wait_send()
-
-        for j, copy in passed_on_extra:
-            copy.wait_send()
+    for edge, n in ((tile > 1, passed[0]), (tile == 1, passed[1])):
+
+        @pl.when(both(helper, edge))
+        def _(n=n):
+            await_bytes(inbox.at[pl.ds(0, n)], z_send.at[1])
+
+
+def scoped(sizes, *refs):
+    dma = pltpu.SemaphoreType.DMA
+    pl.run_scoped(functools.partial(kernel, sizes, *refs), dma((6,)), dma, dma, dma, dma((2,)))
 
 
 def body(sizes, adjoint_new, weights, departure, send_point, block_count, rotation):
@@ -535,7 +538,7 @@
     hbm = pl.BlockSpec(memory_space=pltpu.HBM)
     args = (adjoint_new, weights, departure, send_point, block_count.reshape(-1), rotation.reshape(-1))
     return pl.pallas_call(
-        functools.partial(kernel, sizes),
+        functools.partial(scoped, sizes),
         out_shape=pltpu.VMEM(adjoint_new.shape, F32),
         in_specs=[hbm] * len(args),
         out_specs=pl.BlockSpec(memory_space=pltpu.VMEM),
@@ -552,18 +555,10 @@
             pltpu.VMEM((stencil * groups, LOW), F32),
             pltpu.VMEM((groups * 2 * rows, LOW), F32),
             pltpu.VMEM((blocks, rows + 16, slots), F32),
-            pltpu.VMEM((2 * blocks, rows + 16, slots), F32),
-            pltpu.VMEM((2 * blocks, 8, slots), F32),
-            pltpu.SemaphoreType.DMA((len(args),)),
-            pltpu.SemaphoreType.DMA((n_lev - 1,)),
+            pltpu.VMEM((blocks * (rows + 24) + 3 * (rows + 16), slots), F32),
             pltpu.SemaphoreType.DMA((n_lev,)),
-            pltpu.SemaphoreType.DMA((n_lev,)),
-            pltpu.SemaphoreType.DMA((blocks + 2,)),
             pltpu.SemaphoreType.DMA,
-            pltpu.SemaphoreType.DMA((blocks,)),
-            pltpu.SemaphoreType.DMA((2 * blocks,)),
-            pltpu.SemaphoreType.DMA((blocks, n_lev - 1)),
-            pltpu.SemaphoreType.DMA((2 * blocks,)),
+            pltpu.SemaphoreType.DMA((2,)),
         ],
         compiler_params=pltpu.CompilerParams(
             collective_id=0, has_side_effects=True, vmem_limit_bytes=16 * 1024 * 1024

time: 19.5 us -> 19.1 us (0.979)
  Pallas kernels: 18.6 us -> 18.2 us
    pallas_call x1, Pallas kernels: 18.6 us -> 18.2 us  [body(): pl.pallas_call(functools.partial(scoped, sizes), out_shape=pltpu.VMEM(adj...]
where the time goes in v4:
time: 19.1 us; the launch traced here: 19 us
  Pallas kernels  18.2 us (95%)
  local copies, waits for them, and re-layouts  0.73 us (4%)
    pallas_call x1, Pallas kernels, body(): pl.pallas_call(functools.partial(scoped, sizes), out_shape=pltpu.VMEM(adj...  18.2 us
    unnamed x1, local copies, waits for them, and re-layouts  0.73 us

profile of v4, /device:TPU:8, one launch (start us, length us, event | category | flops | bytes accessed | tf_op | source)
XLA Modules:
  0.0 19.0 jit_solution(10774803176167537180)
XLA Ops:
  0.0 18.2 %shard_map.64 = f32[5,8,2048]{2,1,0:T(8,128)S(1)} custom-call(f32[5,8,2048]{2,1,0:T(8,128)} %refs_0_.1, f32[4,512]{1,0:T(4,128)} %refs_1_.1, s32[4,2048]{1,0:T(4,128)} %refs_2_.1, s32[4,128]{1,0:T(4,128)} %refs_3_.1, s32[4]{0:T(128)} %bitcast.2, s32[2]{0:T(128)} %bitcast.3), custom_call_target="tpu_custom_call" | custom-call | tf_op jit(solution)/shard_map/pallas_call | solution.py:540
  18.2 0.7 %copy.8 = f32[5,8,2048]{2,1,0:T(8,128)} copy(f32[5,8,2048]{2,1,0:T(8,128)S(1)} %shard_map.64) | data formatting | bytes 655360

commit v5 on v4

--- a/solution.py
+++ b/solution.py
@@ -91,6 +91,8 @@
     feeder = jnp.logical_and(even, jnp.logical_not(first))
     second = jnp.logical_and(even, lev == 1)
     other = jnp.logical_and(odd, jnp.logical_not(first))
+    even_panel = lax.rem(panel, 2) == 0
+    odd_panel = jnp.logical_not(even_panel)
     has_prev, has_next = tile > 0, tile < n_tile - 1
     whole = jnp.logical_and(has_prev, has_next)
     yes = tile >= 0
@@ -127,6 +129,12 @@
     def _():
         greet({"tile": next_tile})
 
+        @pl.when(odd_panel)
+        def _():
+            for p in (prev_panel, next_panel):
+                for t in range(2):
+                    greet({"panel": p, "lev": t})
+
     @pl.when(jnp.logical_not(lone))
     def _():
         for d in range(1, n_lev):
@@ -145,9 +153,12 @@
     def _():
         for t in range(1, n_lev):
             greet({"tile": prev_tile, "lev": t})
-        for p in (prev_panel, next_panel):
-            for t in range(2):
-                greet({"panel": p, "tile": prev_tile, "lev": t})
+
+        @pl.when(even_panel)
+        def _():
+            for p in (prev_panel, next_panel):
+                for t in range(2):
+                    greet({"panel": p, "tile": prev_tile, "lev": t})
 
         @pl.when(tile > 1)
         def _():
@@ -230,13 +241,15 @@
             result.append(jnp.where(live[j], weight, 0.0))
         return result
 
+    aslant = jnp.logical_and(lone, odd_panel)
+
     def ahead(j, moved):
         if j >= 2:
             return {**toward[j], "tile": tile + moved}
         return {"tile": toward[j]["tile"] + moved}
 
     def block_copy(j):
-        moved = jnp.where(helper, 1, 0) if j == 1 else (jnp.where(lone, 1, 0) if j >= 2 else 0)
+        moved = jnp.where(helper, 1, 0) if j == 1 else (jnp.where(aslant, 1, 0) if j >= 2 else 0)
         at = j * size if j == 0 else pl.multiple_of(j * size + moved * (blocks * (size + 8) - size), 8)
         return pltpu.make_async_remote_copy(
             src_ref=pay.at[j],
@@ -248,7 +261,7 @@
         )
 
     def extra_copy(j, level):
-        moved = jnp.where(second, 1, 0) if level == 0 and j >= 2 else 0
+        moved = jnp.where(jnp.logical_and(second, odd_panel), 1, 0) if level == 0 and j >= 2 else 0
         return pltpu.make_async_remote_copy(
             src_ref=pay.at[j, pl.ds(at_slot, 8)],
             dst_ref=inbox.at[pl.ds(extras + 8 * j, 8)],
@@ -380,12 +393,19 @@
         inbox.at[pl.ds(aside + size, 2 * size)], inbox.at[last_two], z_send.at[1], p_recv.at[0]
     )
     pass_extras = to_lone(inbox.at[last_extras], inbox.at[last_extras], z_send.at[1], p_recv.at[0])
-    passed = 3 * size + 16, 2 * size + 16
+    passed = [
+        (functools.reduce(jnp.logical_and, (helper, *case)), rows_passed)
+        for case, rows_passed in (
+            ((even_panel, tile > 1), 3 * size + 16),
+            ((even_panel, tile == 1), 2 * size + 16),
+            ((odd_panel, tile > 1), size),
+        )
+    ]
 
     def both(*conditions):
         return functools.reduce(jnp.logical_and, conditions)
 
-    soon = both(feeder, lax.rem(panel, 2) == 0)
+    soon = both(feeder, even_panel, lax.rem(tile, 4) == 0)
 
     def step(i, carry):
         @pl.when(i == jnp.where(helper, 3, jnp.where(other, 1, jnp.where(feeder, 0, -1))))
@@ -428,19 +448,22 @@
         def _():
             await_bytes(w.at[others], w_recv.at[0])
 
-        @pl.when(both(helper, i == 4, tile > 1))
-        def _():
-            await_bytes(inbox.at[pl.ds(0, passed[0])], p_recv.at[1])
-            pass_one.start()
-
-        @pl.when(both(helper, i == 4, tile == 1))
-        def _():
-            await_bytes(inbox.at[pl.ds(0, passed[1])], p_recv.at[1])
+        for case, n in passed:
+
+            @pl.when(both(case, i == 4))
+            def _(n=n):
+                await_bytes(inbox.at[pl.ds(0, n)], p_recv.at[1])
 
         @pl.when(both(helper, i == 4))
         def _():
-            pass_two.start()
-            pass_extras.start()
+            @pl.when(tile > 1)
+            def _():
+                pass_one.start()
+
+            @pl.when(even_panel)
+            def _():
+                pass_two.start()
+                pass_extras.start()
 
         arriving = i == jnp.where(soon, 3, 4)
 
@@ -516,9 +539,9 @@
             result[top : top + rows, :] + result[top + rows : top + 2 * rows, :]
         ).reshape(fields, levels, LOW)
 
-    for edge, n in ((tile > 1, passed[0]), (tile == 1, passed[1])):
-
-        @pl.when(both(helper, edge))
+    for case, n in passed:
+
+        @pl.when(case)
         def _(n=n):
             await_bytes(inbox.at[pl.ds(0, n)], z_send.at[1])
 

time: 19.1 us -> 18.5 us (0.969)
  Pallas kernels: 18.2 us -> 17.7 us
    pallas_call x1, Pallas kernels: 18.2 us -> 17.7 us  [body(): pl.pallas_call(functools.partial(scoped, sizes), out_shape=pltpu.VMEM(adj...]
where the time goes in v5:
time: 18.5 us; the launch traced here: 18.4 us
  Pallas kernels  17.7 us (96%)
  local copies, waits for them, and re-layouts  0.73 us (4%)
    pallas_call x1, Pallas kernels, body(): pl.pallas_call(functools.partial(scoped, sizes), out_shape=pltpu.VMEM(adj...  17.7 us
    unnamed x1, local copies, waits for them, and re-layouts  0.73 us

profile of v5, /device:TPU:8, one launch (start us, length us, event | category | flops | bytes accessed | tf_op | source)
XLA Modules:
  0.0 18.4 jit_solution(6670196719512476071)
XLA Ops:
  0.0 17.7 %shard_map.64 = f32[5,8,2048]{2,1,0:T(8,128)S(1)} custom-call(f32[5,8,2048]{2,1,0:T(8,128)} %refs_0_.1, f32[4,512]{1,0:T(4,128)} %refs_1_.1, s32[4,2048]{1,0:T(4,128)} %refs_2_.1, s32[4,128]{1,0:T(4,128)} %refs_3_.1, s32[4]{0:T(128)} %bitcast.2, s32[2]{0:T(128)} %bitcast.3), custom_call_target="tpu_custom_call" | custom-call | tf_op jit(solution)/shard_map/pallas_call | solution.py:563
  17.7 0.7 %copy.8 = f32[5,8,2048]{2,1,0:T(8,128)} copy(f32[5,8,2048]{2,1,0:T(8,128)S(1)} %shard_map.64) | data formatting | bytes 655360

commit v6 on v5

--- a/solution.py
+++ b/solution.py
@@ -58,6 +58,7 @@
     sent,
     acc,
     pay,
+    mine,
     inbox,
     w_recv,
     r_recv,
@@ -82,6 +83,8 @@
     at_slot = rows + 8
     size = rows + 16
     extras = blocks * size
+    halves = ((1, 3), (0, 2))
+    column = {j: n * slots for n, j in enumerate(halves[0] + halves[1])}
 
     odd = lax.rem(tile, 2) == 1
     even = jnp.logical_not(odd)
@@ -102,7 +105,7 @@
     sends_to = [has_prev, has_next, yes, yes]
     comes_from = [{"tile": next_tile}, {"tile": prev_tile}, {"panel": next_panel}, {"panel": prev_panel}]
     hears = [has_next, has_prev, yes, yes]
-    from_even = [odd, odd, even, even]
+    adds = [jnp.logical_or(jnp.logical_not(first), f) for f in (odd, odd, even, even)]
 
     loads = [
         pltpu.make_async_copy(src, dst, in_sem.at[i])
@@ -145,7 +148,7 @@
             def _(j=j):
                 greet(comes_from[j])
 
-                @pl.when(from_even[j])
+                @pl.when(adds[j])
                 def _():
                     greet({**comes_from[j], "lev": jnp.where(first, 1, 0)})
 
@@ -173,7 +176,7 @@
 
 
     sent_blocks = 2 + has_prev.astype(I32) + has_next.astype(I32)
-    more = jnp.where(lone, n_lev - 1, 0) + jnp.where(second, 1, 0)
+    more = jnp.where(first, n_lev - 1, 0) + jnp.where(second, 1, 0)
 
     def weight_copy(d, dst, sem, device):
         return pltpu.make_async_remote_copy(
@@ -187,7 +190,7 @@
 
     def enter():
         pl.semaphore_wait(barrier, n_lev - 1 + sent_blocks * (1 + more))
-        for d in range(1, n_lev):
+        for d in (2, 3, 1):
             indirect = jnp.logical_and(even, lev == n_lev - d)
 
             @pl.when(indirect)
@@ -214,7 +217,7 @@
     lane = lax.broadcasted_iota(I32, (1, slots), 1)
     live = [lane < count_ref[j] for j in range(blocks)]
     for j in range(blocks):
-        hot[:, j * slots : (j + 1) * slots] = one_hot(point[j] & (LOW - 1), slots)
+        hot[:, column[j] : column[j] + slots] = one_hot(point[j] & (LOW - 1), slots)
 
     def slot_weights(parts):
         lhs = []
@@ -234,7 +237,7 @@
             for n, t in enumerate(parts):
                 for i in range(per_lev):
                     r = n * per_lev + i
-                    piece = found[r * 16 : (r + 1) * 16, j * slots : (j + 1) * slots]
+                    piece = found[r * 16 : (r + 1) * 16, column[j] : column[j] + slots]
                     total = total + jnp.where(cell_high[j] == t * per_lev + i, piece, 0.0)
             own = (row16 & (stencil - 1)) == stencil_of[j]
             weight = jnp.sum(jnp.where(own, total, 0.0), axis=0, keepdims=True)
@@ -255,7 +258,7 @@
             src_ref=pay.at[j],
             dst_ref=inbox.at[pl.ds(at, size)],
             send_sem=p_send,
-            recv_sem=p_recv.at[moved],
+            recv_sem=p_recv.at[jnp.where(moved == 1, 2, j % 2)],
             device_id=ahead(j, moved),
             device_id_type=MESH,
         )
@@ -263,16 +266,16 @@
     def extra_copy(j, level):
         moved = jnp.where(jnp.logical_and(second, odd_panel), 1, 0) if level == 0 and j >= 2 else 0
         return pltpu.make_async_remote_copy(
-            src_ref=pay.at[j, pl.ds(at_slot, 8)],
+            src_ref=mine.at[j] if level else pay.at[j, pl.ds(at_slot, 8)],
             dst_ref=inbox.at[pl.ds(extras + 8 * j, 8)],
             send_sem=e_send,
-            recv_sem=p_recv.at[moved],
+            recv_sem=p_recv.at[jnp.where(moved == 1, 2, j % 2)],
             device_id={**ahead(j, moved), "lev": level},
             device_id_type=MESH,
         )
 
-    def send_blocks():
-        for j in (1, 0, 2, 3):
+    def send_blocks(which=(1, 0, 2, 3)):
+        for j in which:
 
             @pl.when(sends_to[j])
             def _(j=j):
@@ -280,15 +283,19 @@
 
     for j, weight in enumerate(slot_weights([lev])):
         pay[j, at_slot:, :] = jnp.broadcast_to(weight, (8, slots))
-
-    @pl.when(lone)
-    def _():
+        mine[j] = jnp.broadcast_to(weight, (8, slots))
+
+    def send_mine():
         for t in range(1, n_lev):
             for j in (1, 0, 2, 3):
 
                 @pl.when(sends_to[j])
                 def _(j=j, t=t):
                     extra_copy(j, t).start()
+
+    @pl.when(lone)
+    def _():
+        send_mine()
 
     for load in loads[4:]:
         load.wait()
@@ -302,13 +309,21 @@
         glhs[g * height : g * height + 2 * rows, :] = split_rows(part)
         glhs[g * height + 2 * rows : (g + 1) * height, :] = d16
     row8 = lax.broadcasted_iota(I32, (8, slots), 0)
-    for n in range(blocks * slots // LOW):
-        found = jnp.dot(glhs[...], hot[:, n * LOW : (n + 1) * LOW], preferred_element_type=F32)
-        for i in range(LOW // slots):
-            j = n * (LOW // slots) + i
+    some = groups // 2
+    for n, pair in enumerate(halves):
+        found = [
+            jnp.dot(
+                glhs[m * some * height : (m + 1) * some * height, :],
+                hot[:, n * LOW : (n + 1) * LOW],
+                preferred_element_type=F32,
+            )
+            for m in range(2)
+        ]
+        for i, j in enumerate(pair):
             total = jnp.zeros((height, slots), F32)
             for g in range(groups):
-                piece = found[g * height : (g + 1) * height, i * slots : (i + 1) * slots]
+                top = (g % some) * height
+                piece = found[g // some][top : top + height, i * slots : (i + 1) * slots]
                 total = total + jnp.where(cell_high[j] == g, piece, 0.0)
             value = total[:rows] + total[rows : 2 * rows]
             if j >= 2:
@@ -332,14 +347,14 @@
             pay[j, 0:rows, :] = value
             pay[j, rows:at_slot, :] = jnp.broadcast_to(target, (8, slots))
 
-    @pl.when(lone)
-    def _():
-        send_blocks()
+        @pl.when(lone)
+        def _(pair=pair):
+            send_blocks(pair)
 
     number = lax.broadcasted_iota(I32, (stencil * groups, slots), 0)
     marks = [
         jnp.where((number == (point[j] >> shift_low)) & live[j], 1.0, 0.0).astype(BF16)
-        for j in range(blocks)
+        for j in halves[0] + halves[1]
     ]
     sent[...] = times_transposed(jnp.concatenate(marks, axis=1), hot[...])
 
@@ -386,13 +401,24 @@
     others = pl.ds(1, n_lev - 1)
     relay_copy = to_lone(relay.at[others], w.at[others], z_send.at[0], w_recv.at[0])
     aside = blocks * (size + 8)
-    last_two = pl.ds(2 * size, 2 * size)
-    last_extras = pl.ds(extras + 16, 16)
-    pass_one = to_lone(inbox.at[pl.ds(aside, size)], inbox.at[pl.ds(size, size)], z_send.at[1], p_recv.at[0])
-    pass_two = to_lone(
-        inbox.at[pl.ds(aside + size, 2 * size)], inbox.at[last_two], z_send.at[1], p_recv.at[0]
-    )
-    pass_extras = to_lone(inbox.at[last_extras], inbox.at[last_extras], z_send.at[1], p_recv.at[0])
+    pass_on = [
+        to_lone(
+            inbox.at[pl.ds(aside + (j - 1) * size, size)],
+            inbox.at[pl.ds(j * size, size)],
+            z_send.at[1],
+            p_recv.at[j % 2],
+        )
+        for j in range(1, blocks)
+    ]
+    pass_extra = [
+        to_lone(
+            inbox.at[pl.ds(extras + 8 * j, 8)],
+            inbox.at[pl.ds(extras + 8 * j, 8)],
+            z_send.at[1],
+            p_recv.at[j % 2],
+        )
+        for j in (2, 3)
+    ]
     passed = [
         (functools.reduce(jnp.logical_and, (helper, *case)), rows_passed)
         for case, rows_passed in (
@@ -417,17 +443,19 @@
             jnp.where(lone, -1, jnp.where(feeder, 1, 2)),
             jnp.where(lone, -1, jnp.where(soon, 4, 3)),
         )
-        for n in range(3):
+        for n in range(2):
 
             @pl.when(i == when[n])
             def _(n=n):
                 await_bytes(w.at[order[n + 1]], w_recv.at[order[n + 1]])
 
-        @pl.when(both(odd, i == when[2]))
-        def _():
+        @pl.when(both(helper, i == 3))
+        def _():
+            send_mine()
+            await_bytes(w.at[order[3]], w_recv.at[order[3]])
             add_weights(order[1:])
 
-        @pl.when(both(feeder, i == 1))
+        @pl.when(both(jnp.logical_not(first), i == when[1]))
         def _():
             add_weights(order[1:3])
 
@@ -452,18 +480,18 @@
 
             @pl.when(both(case, i == 4))
             def _(n=n):
-                await_bytes(inbox.at[pl.ds(0, n)], p_recv.at[1])
+                await_bytes(inbox.at[pl.ds(0, n)], p_recv.at[2])
 
         @pl.when(both(helper, i == 4))
         def _():
             @pl.when(tile > 1)
             def _():
-                pass_one.start()
+                pass_on[0].start()
 
             @pl.when(even_panel)
             def _():
-                pass_two.start()
-                pass_extras.start()
+                for copy in pass_on[1:] + pass_extra:
+                    copy.start()
 
         arriving = i == jnp.where(soon, 3, 4)
 
@@ -473,6 +501,10 @@
             t = jnp.where(
                 k == 0, order[0], jnp.where(k == 1, order[1], jnp.where(k == 2, order[2], order[3]))
             )
+            @pl.when(both(jnp.logical_not(first), i == when[2]))
+            def _():
+                await_bytes(w.at[0], w_recv.at[0])
+
             acc[...] += segment(t)
 
         @pl.when(arriving)
@@ -484,7 +516,7 @@
                 def _(n=n):
                     await_bytes(pay.at[pl.ds(0, n)], p_send)
 
-                for role, times in ((lone, n_lev - 1), (second, 1)):
+                for role, times in ((first, n_lev - 1), (second, 1)):
 
                     @pl.when(both(role, edge))
                     def _(n=n, times=times):
@@ -494,26 +526,29 @@
             def _():
                 await_bytes(relay.at[others], z_send.at[0])
 
-            for edge, n, m in (
-                (whole, blocks, 2),
-                (jnp.logical_not(has_prev), blocks - 1, 2),
-                (jnp.logical_not(has_next), blocks - 1, 1),
-            ):
-
-                @pl.when(edge)
-                def _(n=n, m=m):
-                    await_bytes(inbox.at[pl.ds(0, n * size + 8 * m)], p_recv.at[0])
-
-            for j in range(blocks):
-
-                @pl.when(jnp.logical_and(hears[j], from_even[j]))
-                def _(j=j):
-                    inbox[j * size + at_slot : (j + 1) * size, :] += inbox[
-                        extras + 8 * j : extras + 8 * (j + 1), :
-                    ]
+            for half, here in ((0, has_next), (1, has_prev)):
+                there = jnp.logical_not(here)
+                for case, n in (
+                    (both(here, first), 2 * size + 8),
+                    (both(here, jnp.logical_not(first)), 2 * size + 16),
+                    (both(there, odd, first), size),
+                    (both(there, jnp.logical_or(even, jnp.logical_not(first))), size + 8),
+                ):
+
+                    @pl.when(case)
+                    def _(n=n, half=half):
+                        await_bytes(inbox.at[pl.ds(0, n)], p_recv.at[half])
+
+                for j in (half, half + 2):
+
+                    @pl.when(jnp.logical_and(hears[j], adds[j]))
+                    def _(j=j):
+                        inbox[j * size + at_slot : (j + 1) * size, :] += inbox[
+                            extras + 8 * j : extras + 8 * (j + 1), :
+                        ]
 
             result = acc[...]
-            for pair in ((0, 2), (1, 3)):
+            for pair in halves:
                 value = jnp.concatenate(
                     [
                         inbox[j * size : j * size + rows, :]
@@ -578,10 +613,11 @@
             pltpu.VMEM((stencil * groups, LOW), F32),
             pltpu.VMEM((groups * 2 * rows, LOW), F32),
             pltpu.VMEM((blocks, rows + 16, slots), F32),
+            pltpu.VMEM((blocks, 8, slots), F32),
             pltpu.VMEM((blocks * (rows + 24) + 3 * (rows + 16), slots), F32),
             pltpu.SemaphoreType.DMA((n_lev,)),
             pltpu.SemaphoreType.DMA,
-            pltpu.SemaphoreType.DMA((2,)),
+            pltpu.SemaphoreType.DMA((3,)),
         ],
         compiler_params=pltpu.CompilerParams(
             collective_id=0, has_side_effects=True, vmem_limit_bytes=16 * 1024 * 1024

time: 18.5 us -> 18.4 us (level)
  no operation moved by 1% of the time
where the time goes in v6:
time: 18.4 us; the launch traced here: 18.3 us
  Pallas kernels  17.6 us (96%)
  local copies, waits for them, and re-layouts  0.73 us (4%)
    pallas_call x1, Pallas kernels, body(): pl.pallas_call(functools.partial(scoped, sizes), out_shape=pltpu.VMEM(adj...  17.6 us
    unnamed x1, local copies, waits for them, and re-layouts  0.73 us

profile of v6, /device:TPU:8, one launch (start us, length us, event | category | flops | bytes accessed | tf_op | source)
XLA Modules:
  0.0 18.3 jit_solution(6016361686124723687)
XLA Ops:
  0.0 17.6 %shard_map.64 = f32[5,8,2048]{2,1,0:T(8,128)S(1)} custom-call(f32[5,8,2048]{2,1,0:T(8,128)} %refs_0_.1, f32[4,512]{1,0:T(4,128)} %refs_1_.1, s32[4,2048]{1,0:T(4,128)} %refs_2_.1, s32[4,128]{1,0:T(4,128)} %refs_3_.1, s32[4]{0:T(128)} %bitcast.2, s32[2]{0:T(128)} %bitcast.3), custom_call_target="tpu_custom_call" | custom-call | tf_op jit(solution)/shard_map/pallas_call | solution.py:598
  17.6 0.7 %copy.8 = f32[5,8,2048]{2,1,0:T(8,128)} copy(f32[5,8,2048]{2,1,0:T(8,128)S(1)} %shard_map.64) | data formatting | bytes 655360

commit v7 on v6

--- a/solution.py
+++ b/solution.py
@@ -281,6 +281,9 @@
             def _(j=j):
                 block_copy(j).start()
 
+    for load in loads[4:]:
+        load.wait()
+
     for j, weight in enumerate(slot_weights([lev])):
         pay[j, at_slot:, :] = jnp.broadcast_to(weight, (8, slots))
         mine[j] = jnp.broadcast_to(weight, (8, slots))
@@ -292,13 +295,6 @@
                 @pl.when(sends_to[j])
                 def _(j=j, t=t):
                     extra_copy(j, t).start()
-
-    @pl.when(lone)
-    def _():
-        send_mine()
-
-    for load in loads[4:]:
-        load.wait()
 
     height = 2 * rows + 16
     for g in range(groups):
@@ -348,8 +344,10 @@
             pay[j, rows:at_slot, :] = jnp.broadcast_to(target, (8, slots))
 
         @pl.when(lone)
-        def _(pair=pair):
+        def _(n=n, pair=pair):
             send_blocks(pair)
+            if n == 0:
+                send_mine()
 
     number = lax.broadcasted_iota(I32, (stencil * groups, slots), 0)
     marks = [

time: 18.4 us -> 18.5 us (level)
  no operation moved by 1% of the time
where the time goes in v7:
time: 18.5 us; the launch traced here: 18.3 us
  Pallas kernels  17.5 us (95%)
  local copies, waits for them, and re-layouts  0.73 us (4%)
    pallas_call x1, Pallas kernels, body(): pl.pallas_call(functools.partial(scoped, sizes), out_shape=pltpu.VMEM(adj...  17.5 us
    unnamed x1, local copies, waits for them, and re-layouts  0.73 us

profile of v7, /device:TPU:8, one launch (start us, length us, event | category | flops | bytes accessed | tf_op | source)
XLA Modules:
  0.0 18.3 jit_solution(10665479738164301505)
XLA Ops:
  0.0 17.5 %shard_map.64 = f32[5,8,2048]{2,1,0:T(8,128)S(1)} custom-call(f32[5,8,2048]{2,1,0:T(8,128)} %refs_0_.1, f32[4,512]{1,0:T(4,128)} %refs_1_.1, s32[4,2048]{1,0:T(4,128)} %refs_2_.1, s32[4,128]{1,0:T(4,128)} %refs_3_.1, s32[4]{0:T(128)} %bitcast.2, s32[2]{0:T(128)} %bitcast.3), custom_call_target="tpu_custom_call" | custom-call | tf_op jit(solution)/shard_map/pallas_call | solution.py:596
  17.5 0.7 %copy.8 = f32[5,8,2048]{2,1,0:T(8,128)} copy(f32[5,8,2048]{2,1,0:T(8,128)S(1)} %shard_map.64) | data formatting | bytes 655360
